TPU v7x, 512 devices: a whole 4x4x16 slice. The times are simulated.
512 devices in a mesh: mem: 16 (over z_hi, y, core), lat: 4 (over x), lon: 8 (over z_lo).
Axes of the slice: x: 4, y: 4, z: 16 (z_hi: 2, z_lo: 8; z = z_hi * 8 + z_lo), core: 2. Of those that a mesh axis runs over, the one named last changes fastest.
Arguments:
- perturbation: bfloat16 [64, 64, 128, 1024], P('mem', None, 'lat', 'lon'), may hold values from -6 to 6
- control: bfloat16 [64, 16, 128, 1024], P('mem', None, 'lat', 'lon'), may hold values from -6 to 6
- filter_length: float32 [16], replicated, may hold values from 20 to 2000
- modes: float32 [64, 16], replicated, may hold values from -1.5 to 1.5
- obs_weights: bfloat16 [16384, 64], P(('lat', 'lon')), may hold values from -1.5 to 1.5
- innovation: float32 [16384], P(('lat', 'lon')), may hold values from -6 to 6
- obs_tile: int32 [16384, 1], P(('lat', 'lon')), may hold values from 0 to 31; in each aligned block of 512 rows (0 to 511, 512 to 1023, ...) at most 32 rows name the same one
- obs_column: int32 [16384], P(('lat', 'lon')), may hold values from 0 to 16383
- obs_count: int32 [32], P(('lat', 'lon')), may hold values from 64 to 512, as said below
Outputs:
- increment: float32 [64, 128, 1024], P('mem', 'lat', 'lon')
- departures: float32 [16384], P(('lat', 'lon'))
Inputs may be any that keep to these rules, and one draw needn't show every extreme that they name: obs_tile names each tile for at most 32 of the 512 slots of one tile, a bound that some block reaches of them. `obs_count`: some tile has all 512 slots live.
All inputs are finite; a program needn't handle non-finite values.
Results may differ from a plain program's by a relative error of at most 0.0003.
Values sent between devices are 32-bit elements; how exact they have to be, the bound alone decides.
A program may use at most 64 MiB of HBM per device.

v0:
```python
import math

import jax
import jax.numpy as jnp
from jax import lax
from jax.sharding import PartitionSpec as P

HIGH = lax.Precision.HIGHEST


def sent_to_all(shard, axis):
    copies = jnp.broadcast_to(shard, (lax.axis_size(axis), *shard.shape))
    return lax.all_to_all(copies, axis, split_axis=0, concat_axis=0, tiled=True)


def collected_together(shard, axis):
    leaves = jax.tree.leaves(shard)
    order = sorted(range(len(leaves)), key=lambda k: -leaves[k].size)
    width = (1, *leaves[order[0]].shape)[-1]
    lines = [
        jnp.pad(leaves[k].reshape(-1), (0, -leaves[k].size % width)).reshape(-1, width)
        for k in order
    ]
    both, at, found = (sent_to_all(jnp.concatenate(lines), axis), 0, {})
    for k, line in zip(order, lines):
        piece = both[:, at : at + len(line)].reshape(len(both), -1)
        found[k] = piece[:, : leaves[k].size].reshape(-1, *leaves[k].shape)
        at += len(line)
    numbers = iter(range(len(leaves)))
    return jax.tree.map(lambda _: found[next(numbers)], shard)


def folded_in_pairs(pieces, combine):
    while len(jax.tree.leaves(pieces)[0]) > 1:
        pieces = jax.vmap(combine)(
            *(jax.tree.map(lambda part: part[side::2], pieces) for side in (0, 1))
        )
    return jax.tree.map(lambda part: part[0], pieces)


def entering(shard, axis, combine, identity):
    peers, here = (lax.axis_size(axis), lax.axis_index(axis))
    passed = jnp.arange(peers) < here

    def entering_kept(part, zero, own):
        part = jnp.where(
            passed.reshape(-1, *(1 for _ in own.shape)), part, jnp.asarray(zero, own.dtype)
        )
        return part

    pieces = collected_together(shard, axis)
    return folded_in_pairs(jax.tree.map(entering_kept, pieces, identity, shard), combine)


def collected_alike(shard, axis):
    leaves, found = (jax.tree.leaves(shard), {})
    for initial, a in enumerate(leaves):
        if initial not in found:
            alike = [k for k, b in enumerate(leaves) if b.dtype == a.dtype]
            got = (
                collected_together([leaves[k] for k in alike], axis)
                if len(alike) > 1
                else [sent_to_all(a, axis)]
            )
            for k, b in zip(alike, got):
                found[k] = b
    numbers = iter(range(len(leaves)))
    return jax.tree.map(lambda _: found[next(numbers)], shard)


def carried_in(shard, axis, combine, identity, reverse):
    peers, here = (lax.axis_size(axis), lax.axis_index(axis))
    passed = jnp.arange(peers) > here if reverse else jnp.arange(peers) < here

    def carried_kept(part, zero, own):
        part = jnp.where(
            passed.reshape(-1, *(1 for _ in own.shape)), part, jnp.asarray(zero, own.dtype)
        )
        return part[::-1] if reverse else part

    pieces = collected_alike(shard, axis)
    return folded_in_pairs(jax.tree.map(carried_kept, pieces, identity, shard), combine)


def cut_along(shard, dim, peers):
    shape = shard.shape
    blocks = shard.reshape(*shape[:dim], peers, shape[dim] // peers, *shape[dim + 1 :])
    return jnp.moveaxis(blocks, dim, 0)


def sum_at_owner(shard, axis, dim):
    blocks = cut_along(shard, dim, lax.axis_size(axis))
    arrived = lax.all_to_all(blocks, axis, split_axis=0, concat_axis=0, tiled=True)
    return arrived.sum(axis=0)


def with_halo(block, sides, width):
    for axis, dim in sides:
        count = lax.axis_size(axis)
        forward = [(i, i + 1) for i in range(count - 1)]
        backward = [(target, source) for source, target in forward]
        low = lax.ppermute(
            lax.slice_in_dim(block, block.shape[dim] - width, None, axis=dim), axis, forward
        )
        high = lax.ppermute(lax.slice_in_dim(block, 0, width, axis=dim), axis, backward)
        block = jnp.concatenate([low, block, high], axis=dim)
    return block


def over_copies(shard, axis):
    everything = sent_to_all(shard, axis)
    return jnp.sum(everything, axis=0)


def filter_matrix(rate, length, backward):
    places = jnp.arange(length)
    if backward:
        spacing = places[None, :] - places[:, None]
    else:
        spacing = places[:, None] - places[None, :]
    inside = spacing >= 0
    powers = jnp.exp(
        jnp.where(inside, spacing, 0).astype(jnp.float32)[None] * jnp.log(rate)[:, None, None]
    )
    return jnp.where(inside[None], (1.0 - rate)[:, None, None] * powers, 0.0)


def carry_factor(rate, length, backward):
    places = jnp.arange(length).astype(jnp.float32)
    steps = length - places if backward else places + 1.0
    return jnp.exp(steps[None, :] * jnp.log(rate)[:, None])


def local_pass(field, rate, dim, backward):
    length = field.shape[dim]
    matrix = filter_matrix(rate, length, backward)
    if dim == 2:
        local = jnp.einsum("kij,mkjy->mkiy", matrix, field, precision=HIGH)
        edge = local[:, :, 0, :] if backward else local[:, :, -1, :]
    else:
        local = jnp.einsum("kij,mkxj->mkxi", matrix, field, precision=HIGH)
        edge = local[:, :, :, 0] if backward else local[:, :, :, -1]
    return (local, edge, jnp.exp(length * jnp.log(rate)))


def settle(local, carry, rate, dim, backward):
    factor = carry_factor(rate, local.shape[dim], backward)
    if dim == 2:
        return local + factor[None, :, :, None] * carry[:, :, None, :]
    return local + factor[None, :, None, :] * carry[:, :, :, None]


def combine(earlier, later):
    return (earlier[0] * later[0], later[0][None, :, None] * earlier[1] + later[1])


def per_device(
    perturbation,
    control,
    filter_length,
    modes,
    obs_weights,
    innovation,
    obs_tile,
    obs_column,
    obs_count,
):
    rate = jnp.exp(-1.0 / filter_length)
    boost = (1.0 + rate) / (1.0 - rate)
    field = control.astype(jnp.float32) * boost[None, :, None, None]
    unity = jnp.ones_like(rate)
    local, edge, whole_power = local_pass(field, rate, 2, False)
    carried = entering((whole_power, edge), "lat", combine, (unity, jnp.zeros_like(edge)))
    field = settle(local, carried[1], rate, 2, False)
    local, edge, whole_power = local_pass(field, rate, 2, True)
    carried = carried_in((whole_power, edge), "lat", combine, (unity, jnp.zeros_like(edge)), True)
    field = settle(local, carried[1], rate, 2, True)
    local, edge, whole_power = local_pass(field, rate, 3, False)
    carried = carried_in((whole_power, edge), "lon", combine, (unity, jnp.zeros_like(edge)), False)
    field = settle(local, carried[1], rate, 3, False)
    local, edge, whole_power = local_pass(field, rate, 3, True)
    carried = carried_in((whole_power, edge), "lon", combine, (unity, jnp.zeros_like(edge)), True)
    field = settle(local, carried[1], rate, 3, True)
    member_count, levels, rows_tile, cols_tile = perturbation.shape
    modes_count = control.shape[1]
    flat_field = field.reshape(member_count, modes_count, rows_tile * cols_tile)
    flat_pert = perturbation.reshape(member_count, levels, rows_tile * cols_tile)
    scaling = 1.0 / math.sqrt(member_count * lax.axis_size("mem") - 1)
    share = levels // lax.axis_size("mem")
    first_level = lax.axis_index("mem") * share
    profile = jnp.einsum("zk,mkp->mzp", modes, flat_field, precision=HIGH)
    owned = sum_at_owner(jnp.sum(flat_pert * profile, axis=0) * scaling, "mem", 0)
    weights_used = lax.dynamic_slice_in_dim(obs_weights, first_level, share, 1).astype(jnp.float32)
    increment = owned.reshape(share, rows_tile, cols_tile)
    depth = owned.shape[0]
    padded = with_halo(owned.reshape(depth, rows_tile, cols_tile), (("lat", 1), ("lon", 2)), 1)
    flat_padded = padded.reshape(depth, (rows_tile + 2) * (cols_tile + 2))
    slots_dev = innovation.shape[0]
    tiles = lax.axis_size(("lat", "lon"))
    capacity = 2 * slots_dev // tiles
    target = obs_tile[:, 0]
    marks = (target[:, None] == jnp.arange(tiles, dtype=jnp.int32)[None, :]).astype(jnp.int32)
    ranking = jnp.sum(jnp.cumsum(marks, axis=0) * marks, axis=1) - 1
    valid = jnp.arange(slots_dev, dtype=jnp.int32) < obs_count[0]
    weight_send = (
        jnp.zeros((tiles, capacity, depth), jnp.float32)
        .at[target, ranking]
        .set(jnp.where(valid[:, None], weights_used, 0.0))
    )
    column_send = (
        jnp.zeros((tiles, capacity), jnp.float32)
        .at[target, ranking]
        .set(obs_column.astype(jnp.float32))
    )
    weights_in = lax.all_to_all(
        weight_send, ("lat", "lon"), split_axis=0, concat_axis=0, tiled=True
    )
    columns_in = lax.all_to_all(
        column_send, ("lat", "lon"), split_axis=0, concat_axis=0, tiled=True
    )
    column_ids = columns_in.astype(jnp.int32)
    fine_row = column_ids // (2 * cols_tile)
    fine_col = column_ids % (2 * cols_tile)
    near_row = fine_row // 2 + 1
    far_row = near_row + 2 * (fine_row % 2) - 1
    near_col = fine_col // 2 + 1
    far_col = near_col + 2 * (fine_col % 2) - 1
    stride = cols_tile + 2
    blend = (
        0.5625 * flat_padded[:, near_row * stride + near_col]
        + 0.1875 * flat_padded[:, far_row * stride + near_col]
        + 0.1875 * flat_padded[:, near_row * stride + far_col]
        + 0.0625 * flat_padded[:, far_row * stride + far_col]
    )
    values = jnp.einsum("tcz,ztc->tc", weights_in, blend, precision=HIGH)
    returned = lax.all_to_all(values, ("lat", "lon"), split_axis=0, concat_axis=0, tiled=True)
    equivalent = returned[target, ranking]
    equivalent = over_copies(equivalent, "mem")
    departures = jnp.where(valid, innovation - equivalent, 0.0)
    return (increment, departures)


def solution(mesh):
    placed = (
        P("mem", None, "lat", "lon"),
        P("mem", None, "lat", "lon"),
        P(),
        P(),
        P(("lat", "lon"), None),
        P(("lat", "lon")),
        P(("lat", "lon"), None),
        P(("lat", "lon")),
        P(("lat", "lon")),
    )
    return jax.shard_map(
        per_device,
        mesh=mesh,
        in_specs=placed,
        out_specs=(P("mem", "lat", "lon"), P(("lat", "lon"))),
        check_vma=False,
    )
```

profile of v0, /device:TPU:1, one launch (start us, length us, event | category | flops | bytes accessed | tf_op | source)
XLA Modules:
  0.0 316.0 jit_solution(1689792812482445537)
XLA Ops:
  1.4 2.3 convolution_bitcast_fusion.4
  4.4 4.8 %all-to-all-start = ((f32[4,65,128]{2,1,0:T(8,128)}), f32[4,65,128]{2,1,0:T(8,128)S(1)}, u32[]{:S(2)}, u32[]{:S(2)}) async-start(f32[4,65,128]{2,1,0:T(8,128)} %broadcast_in_dim.213), calls=%async_computation | async-start | bytes 294912 | tf_op jit(solution)/shard_map/all_to_all | solution.py:13
  11.1 3.0 all-to-all-done
  16.6 3.3 %all-to-all-start.1 = ((f32[4,65,128]{2,1,0:T(8,128)}), f32[4,65,128]{2,1,0:T(8,128)S(1)}, u32[]{:S(2)}, u32[]{:S(2)}) async-start(f32[4,65,128]{2,1,0:T(8,128)} %broadcast_in_dim.219), calls=%async_computation.1 | async-start | bytes 294912 | tf_op jit(solution)/shard_map/all_to_all | solution.py:13
  19.9 4.9 %all-to-all-done.1 = f32[4,65,128]{2,1,0:T(8,128)S(1)} async-done(((f32[4,65,128]{2,1,0:T(8,128)}), f32[4,65,128]{2,1,0:T(8,128)S(1)}, u32[]{:S(2)}, u32[]{:S(2)}) %all-to-all-start.1) | async-done | bytes 133152 | tf_op jit(solution)/shard_map/all_to_all | solution.py:13
  25.3 2.5 convolution_bitcast_fusion.2
  29.4 12.2 %all-to-all-start.2 = ((f32[8,65,32]{1,2,0:T(8,128)}), f32[8,65,32]{1,2,0:T(8,128)S(1)}, u32[]{:S(2)}, u32[]{:S(2)}) async-start(f32[8,65,32]{1,2,0:T(8,128)} %broadcast_in_dim.224), calls=%async_computation.2 | async-start | bytes 262144 | tf_op jit(solution)/shard_map/all_to_all | solution.py:13
  41.8 10.2 %all-to-all-done.2 = f32[8,65,32]{1,2,0:T(8,128)S(1)} async-done(((f32[8,65,32]{1,2,0:T(8,128)}), f32[8,65,32]{1,2,0:T(8,128)S(1)}, u32[]{:S(2)}, u32[]{:S(2)}) %all-to-all-start.2) | async-done | bytes 66592 | tf_op jit(solution)/shard_map/all_to_all | solution.py:13
  52.9 2.5 convolution_bitcast_fusion.1
  56.7 3.4 %all-to-all-start.3 = ((f32[8,65,32]{1,2,0:T(8,128)}), f32[8,65,32]{1,2,0:T(8,128)S(1)}, u32[]{:S(2)}, u32[]{:S(2)}) async-start(f32[8,65,32]{1,2,0:T(8,128)} %broadcast_in_dim.230), calls=%async_computation.3 | async-start | bytes 262144 | tf_op jit(solution)/shard_map/all_to_all | solution.py:13
  60.1 4.5 %reshape.699 = f32[4,64,4096]{2,1,0:T(8,128)} reshape(bf16[4,64,32,128]{3,2,1,0:T(8,128)(2,1)} %param.9) | data formatting | bytes 6291456 | tf_op jit(solution)/shard_map/convert_element_type | solution.py:192
  65.3 67.7 %scatter_fusion.1 = f32[32,32]{1,0:T(8,128)} fusion(f32[32,32]{1,0:T(8,128)} %broadcast_in_dim.235, s32[512]{0:T(512)S(1)} %bitcast.130, f32[512]{0:T(512)S(1)} %convert_element_type.116), kind=kCustom, calls=%fused_computation.6 | custom fusion | bytes 10240 | tf_op jit(solution)/shard_map/scatter | solution.py:213
  132.9 10.8 %all-to-all-start.6 = ((f32[32,1,32]{2,1,0:T(1,128)}), f32[32,1,32]{2,1,0:T(1,128)S(1)}, u32[]{:S(2)}, u32[]{:S(2)}) async-start(f32[32,1,32]{2,1,0:T(1,128)} %bitcast.45), calls=%async_computation.6 | async-start | bytes 32768 | tf_op jit(solution)/shard_map/all_to_all | solution.py:218
  145.5 5.5 %fusion.1 = f32[64,4096]{1,0:T(8,128)S(1)} fusion(f32[4,64,4096]{2,1,0:T(8,128)} %reshape.699, f32[4,16,4096]{2,0,1:T(4,128)S(1)} %reshape.695, f32[64,16]{0,1:T(8,128)S(1)} %copy-done), kind=kOutput, calls=%fused_computation.9 | convolution fusion | flops 203161600 | bytes 6295552 | tf_op jit(solution)/shard_map/zk,mkp->mzp/dot_general | solution.py:191
  152.4 2.5 all-to-all-done.6
  154.9 16.5 %all-to-all-start.4 = ((f32[16,4,4096]{2,1,0:T(4,128)}), f32[16,4,4096]{2,1,0:T(4,128)S(1)}, u32[]{:S(2)}, u32[]{:S(2)}) async-start(f32[16,4,4096]{2,1,0:T(4,128)} %mul.496), calls=%async_computation.4 | async-start | bytes 2097152 | tf_op jit(solution)/shard_map/all_to_all | solution.py:93
  173.0 24.2 %scatter_fusion = f32[32,32,4]{2,1,0:T(8,128)S(1)} fusion(f32[32,32,4]{2,1,0:T(8,128)S(1)} %broadcast_in_dim.232, s32[512]{0:T(512)S(1)} %bitcast.131, f32[512,4]{1,0:T(8,128)S(1)} %copy.190), kind=kCustom, calls=%fused_computation.5 | custom fusion | bytes 28672 | tf_op jit(solution)/shard_map/scatter | solution.py:208
  198.6 1.8 all-to-all-done.4
  200.4 37.0 %all-to-all-start.5 = ((f32[32,1,128]{2,1,0:T(1,128)}), f32[32,1,128]{2,1,0:T(1,128)S(1)}, u32[]{:S(2)}, u32[]{:S(2)}) async-start(f32[32,1,128]{2,1,0:T(1,128)} %reshape.774), calls=%async_computation.5 | async-start | bytes 32768 | tf_op jit(solution)/shard_map/all_to_all | solution.py:215
  237.6 3.1 collective-permute-start
  240.7 1.3 collective-permute-start.1
  242.1 3.2 %collective-permute-done.1 = f32[4,1,128]{2,1,0:T(1,128)S(1)} collective-permute-done((f32[4,1,128]{2,1,0:T(1,128)S(1)}, f32[4,1,128]{2,1,0:T(1,128)S(1)}, u32[]{:S(2)}, u32[]{:S(2)}) %collective-permute-start.1) | collective-permute-done | bytes 2080 | tf_op jit(solution)/shard_map/ppermute | solution.py:105
  245.5 3.1 collective-permute-start.2
  248.6 1.3 collective-permute-start.3
  251.2 2.5 collective-permute-done.3
  254.7 2.8 gather_fusion
  257.8 2.8 gather_fusion.1
  260.8 2.8 gather_fusion.2
  263.8 2.8 gather_fusion.3
  267.0 21.7 %all_to_all.57 = f32[32,1,32]{2,1,0:T(1,128)S(1)} all-to-all(f32[32,1,32]{2,1,0:T(1,128)S(1)} %bitcast.151), channel_id=1, replica_groups=mesh['mem'=16,'lat'=4,'lon'=8] {'lat','lon'}, dimensions={0} | all-to-all | bytes 8192 | tf_op jit(solution)/shard_map/all_to_all | solution.py:236
  288.7 3.8 %gather_fusion.4 = f32[512]{0:T(512)S(1)} fusion(f32[32,32]{1,0:T(8,128)S(1)} %bitcast.129, s32[512]{0:T(512)S(1)} %bitcast.132), kind=kCustom, calls=%fused_computation.4 | custom fusion | bytes 8192 | tf_op jit(solution)/shard_map/gather | solution.py:237
  292.5 22.9 %all_to_all.58 = f32[16,1,512]{2,1,0:T(1,128)S(1)} all-to-all(f32[16,1,512]{2,1,0:T(1,128)S(1)} %broadcast_in_dim.236), channel_id=1, replica_groups=mesh['mem'=16,'lat'=4,'lon'=8] {'mem'}, dimensions={0} | all-to-all | bytes 65536 | tf_op jit(solution)/shard_map/all_to_all | solution.py:13
  (162 shorter events, 19.9 us)
Async XLA Ops:
  0.6 144.9 %copy-start = (f32[64,16]{0,1:T(8,128)S(1)}, f32[64,16]{0,1:T(8,128)}, u32[]{:S(2)}) copy-start(f32[64,16]{0,1:T(8,128)} %param.12) | copy-start | bytes 12292
  0.6 8.8 %copy-start.2 = (s32[512,1]{0,1:T(1,128)S(1)}, s32[512,1]{0,1:T(1,128)}, u32[]{:S(2)}) copy-start(s32[512,1]{0,1:T(1,128)} %param.15) | copy-start | bytes 6148
  4.4 9.7 %all-to-all-start = ((f32[4,65,128]{2,1,0:T(8,128)}), f32[4,65,128]{2,1,0:T(8,128)S(1)}, u32[]{:S(2)}, u32[]{:S(2)}) async-start(f32[4,65,128]{2,1,0:T(8,128)} %broadcast_in_dim.213), calls=%async_computation | async-start | bytes 294912 | tf_op jit(solution)/shard_map/all_to_all | solution.py:13
  16.6 8.2 %all-to-all-start.1 = ((f32[4,65,128]{2,1,0:T(8,128)}), f32[4,65,128]{2,1,0:T(8,128)S(1)}, u32[]{:S(2)}, u32[]{:S(2)}) async-start(f32[4,65,128]{2,1,0:T(8,128)} %broadcast_in_dim.219), calls=%async_computation.1 | async-start | bytes 294912 | tf_op jit(solution)/shard_map/all_to_all | solution.py:13
  29.4 22.5 %all-to-all-start.2 = ((f32[8,65,32]{1,2,0:T(8,128)}), f32[8,65,32]{1,2,0:T(8,128)S(1)}, u32[]{:S(2)}, u32[]{:S(2)}) async-start(f32[8,65,32]{1,2,0:T(8,128)} %broadcast_in_dim.224), calls=%async_computation.2 | async-start | bytes 262144 | tf_op jit(solution)/shard_map/all_to_all | solution.py:13
  56.7 76.3 %all-to-all-start.3 = ((f32[8,65,32]{1,2,0:T(8,128)}), f32[8,65,32]{1,2,0:T(8,128)S(1)}, u32[]{:S(2)}, u32[]{:S(2)}) async-start(f32[8,65,32]{1,2,0:T(8,128)} %broadcast_in_dim.230), calls=%async_computation.3 | async-start | bytes 262144 | tf_op jit(solution)/shard_map/all_to_all | solution.py:13
  60.1 4.5 %copy-start.3 = (s32[512]{0:T(512)S(1)}, s32[512]{0:T(512)}, u32[]{:S(2)}) copy-start(s32[512]{0:T(512)} %param.16) | copy-start | bytes 6148
  132.9 22.0 %all-to-all-start.6 = ((f32[32,1,32]{2,1,0:T(1,128)}), f32[32,1,32]{2,1,0:T(1,128)S(1)}, u32[]{:S(2)}, u32[]{:S(2)}) async-start(f32[32,1,32]{2,1,0:T(1,128)} %bitcast.45), calls=%async_computation.6 | async-start | bytes 32768 | tf_op jit(solution)/shard_map/all_to_all | solution.py:218
  154.9 45.5 %all-to-all-start.4 = ((f32[16,4,4096]{2,1,0:T(4,128)}), f32[16,4,4096]{2,1,0:T(4,128)S(1)}, u32[]{:S(2)}, u32[]{:S(2)}) async-start(f32[16,4,4096]{2,1,0:T(4,128)} %mul.496), calls=%async_computation.4 | async-start | bytes 2097152 | tf_op jit(solution)/shard_map/all_to_all | solution.py:93
  200.4 49.5 %all-to-all-start.5 = ((f32[32,1,128]{2,1,0:T(1,128)}), f32[32,1,128]{2,1,0:T(1,128)S(1)}, u32[]{:S(2)}, u32[]{:S(2)}) async-start(f32[32,1,128]{2,1,0:T(1,128)} %reshape.774), calls=%async_computation.5 | async-start | bytes 32768 | tf_op jit(solution)/shard_map/all_to_all | solution.py:215
  237.6 20.2 %copy-start.1 = (f32[1,4,32,128]{3,2,1,0:T(8,128)}, f32[1,4,32,128]{3,2,1,0:T(8,128)S(1)}, u32[]{:S(2)}) copy-start(f32[1,4,32,128]{3,2,1,0:T(8,128)S(1)} %copy.229) | copy-start | bytes 196612
  237.6 4.5 %collective-permute-start = (f32[4,1,128]{2,1,0:T(1,128)S(1)}, f32[4,1,128]{2,1,0:T(1,128)S(1)}, u32[]{:S(2)}, u32[]{:S(2)}) collective-permute-start(f32[4,1,128]{2,1,0:T(1,128)S(1)} %get-tuple-element.16), channel_id=1, source_target_pairs={{0,8},{8,16},{16,24},{1,9},{9,17},{17,25},{2,10},{10,18},{18,26},{... | collective-permute-start | bytes 6152 | tf_op jit(solution)/shard_map/ppermute | solution.py:102
  240.7 4.6 %collective-permute-start.1 = (f32[4,1,128]{2,1,0:T(1,128)S(1)}, f32[4,1,128]{2,1,0:T(1,128)S(1)}, u32[]{:S(2)}, u32[]{:S(2)}) collective-permute-start(f32[4,1,128]{2,1,0:T(1,128)S(1)} %get-tuple-element.17), channel_id=1, source_target_pairs={{8,0},{16,8},{24,16},{9,1},{17,9},{25,17},{10,2},{18,10},{26,18},{... | collective-permute-start | bytes 6152 | tf_op jit(solution)/shard_map/ppermute | solution.py:105
  245.5 5.7 %collective-permute-start.2 = (f32[4,34,1]{2,1,0:T(8,128)S(1)}, f32[4,34,1]{2,1,0:T(8,128)S(1)}, u32[]{:S(2)}, u32[]{:S(2)}) collective-permute-start(f32[4,34,1]{2,1,0:T(8,128)S(1)} %get-tuple-element.14), channel_id=1, source_target_pairs={{0,1},{1,2},{2,3},{3,4},{4,5},{5,6},{6,7},{8,9},{9,10},{10,11},{11... | collective-permute-start | bytes 1640 | tf_op jit(solution)/shard_map/ppermute | solution.py:102
  248.6 5.2 %collective-permute-start.3 = (f32[4,34,1]{2,1,0:T(8,128)S(1)}, f32[4,34,1]{2,1,0:T(8,128)S(1)}, u32[]{:S(2)}, u32[]{:S(2)}) collective-permute-start(f32[4,34,1]{2,1,0:T(8,128)S(1)} %get-tuple-element.15), channel_id=1, source_target_pairs={{1,0},{2,1},{3,2},{4,3},{5,4},{6,5},{7,6},{9,8},{10,9},{11,10},{12... | collective-permute-start | bytes 1640 | tf_op jit(solution)/shard_map/ppermute | solution.py:105
  263.6 51.8 %copy-start.4 = (f32[512]{0:T(512)S(1)}, f32[512]{0:T(512)}, u32[]{:S(2)}) copy-start(f32[512]{0:T(512)} %param.14) | copy-start | bytes 6148
where the time goes:
time: 318 us; the launch traced here: 316 us
  local copies, waits for them, and re-layouts  123 us (39%)
  starting transfers between devices  97 us (31%)
  blocking collectives  44.6 us (14%)
  waiting for transfers between devices  28.2 us (9%)
  matrix products  14 us (4%)
  other arithmetic  6.94 us (2%)
    scatter x1, local copies, waits for them, and re-layouts, per_device(): column_send = jnp.zeros((tiles, capacity), jnp.float32).at[target, rankin...  67.7 us
    all_to_all x1, starting transfers between devices, per_device(): lax.all_to_all(weight_send, ('lat', 'lon'), split_axis=0, concat_axis=0,...  37 us
    scatter x2, local copies, waits for them, and re-layouts, per_device(): weight_send = jnp.zeros((tiles, capacity, depth), jnp.float32).at[target,...  24.5 us
    all_to_all x4, starting transfers between devices, sent_to_all(): return lax.all_to_all(copies, axis, split_axis=0, concat_axis=0, tiled=True)  23.8 us
    all_to_all x1, blocking collectives, sent_to_all(): return lax.all_to_all(copies, axis, split_axis=0, concat_axis=0, tiled=True)  22.9 us
    all_to_all x1, blocking collectives, per_device(): lax.all_to_all(values, ('lat', 'lon'), split_axis=0, concat_axis=0, tiled...  21.7 us
    all_to_all x4, waiting for transfers between devices, sent_to_all(): return lax.all_to_all(copies, axis, split_axis=0, concat_axis=0, tiled=True)  18.1 us
    all_to_all x1, starting transfers between devices, sum_at_owner(): lax.all_to_all(blocks, axis, split_axis=0, concat_axis=0, tiled=True)  16.5 us
  transfers between devices with their start and end apart: 11, of which 7 were waited for; matrix products, arithmetic and copies ran while one was open for 35% of the time, Pallas kernels for 0%

commit v1 on v0

v1 whole, which is shorter than its diff:
```python
import math

import jax
import jax.numpy as jnp
from jax import lax
from jax.experimental import pallas as pl
from jax.experimental.pallas import tpu as pltpu
from jax.sharding import PartitionSpec as P

F32, BF16, I32 = jnp.float32, jnp.bfloat16, jnp.int32
MESH = pl.DeviceIdType.MESH
ZH, Y, C = 2, 4, 2
LAT, LON = 4, 8
NX, NY, TX, TY = 128, 1024, 32, 128
TILES = LAT * LON


def iota(shape, dim):
    return lax.broadcasted_iota(I32, shape, dim)


def halves(v):
    high = v.astype(BF16)
    return high, (v - high.astype(F32)).astype(BF16)


def thirds(v):
    high, rest = v.astype(BF16), v - v.astype(BF16).astype(F32)
    return (high, *halves(rest))


def dot(a, b):
    return lax.dot_general(a, b, (((1,), (0,)), ((), ())), preferred_element_type=F32)


def dot_nt(a, b):
    return lax.dot_general(a, b, (((1,), (1,)), ((), ())), preferred_element_type=F32)


def dot_tn(a, b):
    return lax.dot_general(a, b, (((0,), (0,)), ((), ())), preferred_element_type=F32)


def kernel(
    il_b, il_kx, modes, weights, innovation, tgt, col, count, ctrl_hbm, pert_hbm,
    inc_ref, dep_ref,
    ctrl, pert, field, lat_send, lat_recv, lon_send, lon_recv, pk_send, pk_recv,
    total, core_recv, red1, y_recv, red2, z_recv,
    row_send, row_recv, edge_send, edge_recv, val, val_recv, vsum, yc_recv, vsum2, x_recv,
    load_sem, lat_s, lat_r, lon_s, lon_r, pk_s, pk_r, core_s, core_r, y_s, y_r, z_s, z_r,
    row_s, row_r, edge_s, edge_r, val_s, val_r, yc_s, yc_r, x_s, x_r,
):
    mem, a, b = (lax.axis_index(n) for n in ("mem", "lat", "lon"))
    zh, y, c = mem // (Y * C), (mem // C) % Y, mem % C
    q = y * C + c

    def remote(src, dst, s, r, dev):
        return pltpu.make_async_remote_copy(
            src_ref=src, dst_ref=dst, send_sem=s, recv_sem=r, device_id=dev, device_id_type=MESH
        )

    load_c = pltpu.make_async_copy(ctrl_hbm, ctrl, load_sem.at[0])
    load_p = pltpu.make_async_copy(pert_hbm, pert, load_sem.at[1])
    load_c.start()
    load_p.start()
    row_recv[...] = jnp.zeros_like(row_recv)
    edge_recv[...] = jnp.zeros_like(edge_recv)

    barrier = pltpu.get_barrier_semaphore()

    def greet(dev):
        pl.semaphore_signal(barrier, inc=1, device_id=dev, device_id_type=MESH)

    for d in range(1, TILES):
        greet((mem, (a + d // LON) % LAT, (b + d % LON) % LON))
    for d in range(1, Y * C):
        greet((zh * Y * C + (q + d) % (Y * C), a, b))
    for d in range(LON):
        greet(((mem + Y * C) % (ZH * Y * C), a, (b + d) % LON))

    rest_x = (NX - TX * a).astype(F32)
    rest_y = (NY - TY * b).astype(F32)
    load_c.wait()
    for g in range(2):
        il = il_kx[0:1, g * 256 : (g + 1) * 256]
        rows, cols = iota((16, 256), 0), iota((16, 256), 1)
        x = (cols & 31).astype(F32)
        up = jnp.exp((x - 31.0) * il)
        down = jnp.exp(-x * il) - jnp.exp((x - 2.0 * rest_x) * il)
        table = jnp.where(cols >> 5 == (rows & 7), jnp.where(rows < 8, up, down), 0.0)
        high, low = halves(table)
        for m in range(4):
            s = ctrl[m, g * 8 : (g + 1) * 8].reshape(256, 128)
            e = dot(high, s) + dot(low, s)
            lat_send[0, m, g * 8 : (g + 1) * 8, :] = e[0:8]
            lat_send[1, m, g * 8 : (g + 1) * 8, :] = e[8:16]

    pl.semaphore_wait(barrier, TILES - 1 + Y * C - 1 + LON)
    lat_copies = []
    for d in range(1, LAT):
        copy = remote(
            lat_send.at[(a + d) // LAT], lat_recv.at[d - 1], lat_s.at[d - 1], lat_r.at[d - 1],
            (mem, (a + d) % LAT, b),
        )
        copy.start()
        lat_copies.append(copy)

    for g in range(2):
        il = il_kx[0:1, g * 256 : (g + 1) * 256]
        rows, cols = iota((256, 256), 0), iota((256, 256), 1)
        x1, x2 = (rows & 31).astype(F32), (cols & 31).astype(F32)
        near = jnp.exp(-jnp.abs(x1 - x2) * il)
        back = jnp.exp((x1 + x2 - 2.0 * rest_x) * il)
        high, low = halves(jnp.where(rows >> 5 == cols >> 5, near - back, 0.0))
        for m in range(4):
            s = ctrl[m, g * 8 : (g + 1) * 8].reshape(256, 128)
            out = dot(high, s) + dot(low, s)
            field[g * 8 : (g + 1) * 8, m * TX : (m + 1) * TX, :] = out.reshape(8, TX, TY)

    t = tgt[...]
    rel = (((t >> 3) + (LAT - a)) & 3) * LON + (((t & 7) + (LON - b)) & 7)
    marks = jnp.where(iota((TILES, 512), 0) == rel, 1.0, 0.0)
    before = jnp.where(iota((512, 512), 0) < iota((512, 512), 1), 1.0, 0.0).astype(BF16)
    rank = jnp.sum(dot(marks.astype(BF16), before) * marks, axis=0, keepdims=True).astype(I32)
    slot = rel * 32 + rank
    chosen = jnp.where(iota((1024, 512), 0) == slot, 1.0, 0.0).astype(BF16)
    r8 = iota((8, 64), 0)
    level = (r8 >> 2) * 32 + q * 4 + (r8 & 3)
    own = jnp.where(iota((8, 64), 1) == level, 1.0, 0.0).astype(BF16)
    picked = dot_nt(own, weights[...])
    place = col[...]
    r8 = iota((8, 512), 0)
    places = jnp.where(r8 == 0, (place >> 7).astype(F32), (place & 127).astype(F32))
    packed = dot_nt(jnp.concatenate([picked, places], 0).astype(BF16), chosen)
    spot = jnp.broadcast_to(packed[8:9] * 128.0 + packed[9:10], (8, 1024))
    lane = iota((8, 128), 1)
    for k in range(TILES):
        block, j = slice(k // 4 * 128, k // 4 * 128 + 128), k % 4
        w = packed[0:8, block]
        p = spot[:, block]
        w = pltpu.roll(w, (128 - 32 * j) % 128, 1) if j else w
        p = pltpu.roll(p, (160 - 32 * j) % 128, 1) if j != 1 else p
        tile = jnp.where(lane < 32, w, p)
        if k:
            pk_send[k] = tile
        else:
            pk_recv[0] = tile

    ilb = il_b[...]
    carry_l, carry_r = [0.0] * 4, [0.0] * 4
    for d in range(1, LAT):
        lat_copies[d - 1].wait_recv()
        left = jnp.where(a >= d, 1.0, 0.0)
        wl = jnp.exp(-32.0 * (d - 1) * ilb) * left
        wr = jnp.exp(-32.0 * (LAT - 1 - d) * ilb) * (1.0 - left)
        for m in range(4):
            got = lat_recv[d - 1, m]
            carry_l[m] = carry_l[m] + wl * got
            carry_r[m] = carry_r[m] + wr * got
    x = iota((TX, TY), 0).astype(F32)
    ly = iota((8, TY), 1).astype(F32)
    r8 = iota((8, TY), 0)
    for k in range(16):
        il = ilb[k : k + 1]
        ahead = jnp.exp(-(x + 1.0) * il) - jnp.exp((x - 1.0 - 2.0 * rest_x) * il)
        behind = jnp.exp((x - 32.0) * il)
        for m in range(4):
            here = slice(m * TX, (m + 1) * TX)
            field[k, here, :] = (
                field[k, here, :] + ahead * carry_l[m][k : k + 1] + behind * carry_r[m][k : k + 1]
            )
        up = jnp.exp((ly - 127.0) * il)
        down = jnp.exp(-ly * il) - jnp.exp((ly - 2.0 * rest_y) * il)
        th, tl = halves(jnp.where(r8 == 0, up, down))
        fh, fl = halves(field[k])
        e = dot_nt(th, fh) + dot_nt(th, fl) + dot_nt(tl, fh)
        lon_send[0, k : k + 1, :] = e[0:1]
        lon_send[1, k : k + 1, :] = e[1:2]
    lon_copies = []
    for d in range(1, LON):
        copy = remote(
            lon_send.at[(b + d) // LON], lon_recv.at[d - 1], lon_s.at[d - 1], lon_r.at[d - 1],
            (mem, a, (b + d) % LON),
        )
        copy.start()
        lon_copies.append(copy)

    y1, y2 = iota((TY, TY), 0).astype(F32), iota((TY, TY), 1).astype(F32)
    for k in range(16):
        il = ilb[k : k + 1]
        nh, nl = halves(
            jnp.exp(-jnp.abs(y1 - y2) * il) - jnp.exp((y1 + y2 - 2.0 * rest_y) * il)
        )
        fh, fl = halves(field[k])
        field[k] = dot(fh, nh) + dot(fl, nh) + dot(fh, nl)

    spread = jnp.where(iota((512, 64), 0) >> 3 == iota((512, 64), 1), 1.0, 0.0).astype(BF16)
    widen = jnp.where(iota((16, 128), 0) == iota((16, 128), 1) >> 3, 1.0, 0.0).astype(BF16)
    diagonal = (iota((512, 128), 0) & 7) == (iota((512, 128), 1) & 7)
    mh, ml = (
        jnp.where(diagonal, dot(dot(spread, part).astype(BF16), widen), 0.0).astype(BF16)
        for part in halves(modes[...])
    )

    cl, cr = 0.0, 0.0
    for d in range(1, LON):
        lon_copies[d - 1].wait_recv()
        left = jnp.where(b >= d, 1.0, 0.0)
        got = lon_recv[d - 1]
        cl = cl + (jnp.exp(-128.0 * (d - 1) * ilb) * left) * got
        cr = cr + (jnp.exp(-128.0 * (LON - 1 - d) * ilb) * (1.0 - left)) * got
    pk_copies = []
    for k in range(1, TILES):
        copy = remote(
            pk_send.at[k], pk_recv.at[k], pk_s.at[k - 1], pk_r.at[k - 1],
            (mem, (a + k // LON) % LAT, (b + k % LON) % LON),
        )
        copy.start()
        pk_copies.append(copy)
    for k in range(16):
        il = ilb[k : k + 1]
        ahead = jnp.exp(-(ly + 1.0) * il) - jnp.exp((ly - 1.0 - 2.0 * rest_y) * il)
        behind = jnp.exp((ly - 128.0) * il)
        ah, al = halves(jnp.where(r8 == 0, ahead, jnp.where(r8 == 1, behind, 0.0)))
        ch, co = halves(
            jnp.where(r8 == 0, cl[k : k + 1], jnp.where(r8 == 1, cr[k : k + 1], 0.0))
        )
        field[k] = field[k] + (dot_tn(ch, ah) + dot_tn(co, ah) + dot_tn(ch, al))

    load_p.wait()
    for xb in range(4):
        acc = None
        for m in range(4):
            rows = field[:, m * TX + xb * 8 : m * TX + xb * 8 + 8, :].reshape(128, 128)
            fh, fl = halves(rows)
            prof = dot(mh, fh) + dot(mh, fl) + dot(ml, fh)
            p = pert[m, :, xb * 8 : xb * 8 + 8, :].astype(F32).reshape(512, 128)
            acc = prof * p if acc is None else acc + prof * p
        total[:, :, :, xb * 8 : xb * 8 + 8, :] = acc.reshape(8, 2, 4, 8, 128)

    core_copy = remote(
        total.at[:, 1 - c], core_recv, core_s.at[0], core_r.at[0], (mem + 1 - 2 * c, a, b)
    )
    core_copy.start()
    core_copy.wait_recv()
    red1[...] = (total[:, c] + core_recv[...]).reshape(2, 4, 4, TX, TY)
    y_copies = []
    for d in range(1, Y):
        yp = (y + d) % Y
        copy = remote(
            red1.at[:, yp], y_recv.at[d - 1], y_s.at[d - 1], y_r.at[d - 1],
            ((zh * Y + yp) * C + c, a, b),
        )
        copy.start()
        y_copies.append(copy)

    w_all, p_all = jnp.zeros((64, 128), F32), jnp.zeros((64, 128), F32)
    group = iota((64, 128), 1) >> 5
    for da in range(LAT):
        for k in range(max(1, da * LON), (da + 1) * LON):
            pk_copies[k - 1].wait_recv()
        got = pk_recv[da * LON : (da + 1) * LON].reshape(64, 128)
        w = pltpu.roll(got, 32 * da, 1) if da else got
        p = pltpu.roll(got, (32 * da + 96) % 128, 1) if da != 1 else got
        w_all = jnp.where(group == da, w, w_all)
        p_all = jnp.where(group == da, p, p_all)

    for copy in y_copies:
        copy.wait_recv()
    whole = red1[:, y] + y_recv[0] + y_recv[1] + y_recv[2]
    whole = whole.reshape(8, TX, TY)
    red2[...] = whole
    z_copy = remote(
        red2.at[pl.ds((1 - zh) * 4, 4)], z_recv, z_s.at[0], z_r.at[0],
        ((mem + Y * C) % (ZH * Y * C), a, b),
    )

    r8 = iota((8, 128), 0)
    ends = jnp.where(
        (r8 == 0) & (lane == 0) | (r8 == 1) & (lane == 127), 1.0, 0.0
    ).astype(BF16)
    wh, wl = halves(whole.reshape(256, 128))
    row_send[0] = red2[:, TX - 1, :]
    row_send[1] = red2[:, 0, :]
    edge_send[...] = dot_nt(ends, wh) + dot_nt(ends, wl)
    halo = []
    for s in range(2):
        step = 1 - 2 * s
        copy = remote(
            row_send.at[s], row_recv.at[s], row_s.at[s], row_r.at[s],
            (mem, (a + step + LAT) % LAT, b),
        )
        there, back = a + step, a - step
        halo.append((copy, (there >= 0) & (there < LAT), (back >= 0) & (back < LAT)))
    for i, da in enumerate((-1, 0, 1)):
        for j, db in enumerate((-1, 1)):
            copy = remote(
                edge_send, edge_recv.at[i, j], edge_s.at[i, j], edge_r.at[i, j],
                (mem, (a - da + LAT) % LAT, (b - db + LON) % LON),
            )
            at, bt, af, bf = a - da, b - db, a + da, b + db
            halo.append((
                copy,
                (at >= 0) & (at < LAT) & (bt >= 0) & (bt < LON),
                (af >= 0) & (af < LAT) & (bf >= 0) & (bf < LON),
            ))
    for copy, sends, _ in halo:
        pl.when(sends)(copy.start)
    z_copy.start()
    for copy, _, gets in halo:
        pl.when(gets)(copy.wait_recv)

    top, bottom = halves(row_recv[0]), halves(row_recv[1])
    r8w = iota((8, 256), 0)
    l8w = iota((8, 256), 1)

    def sides(i):
        both = jnp.where(
            r8w % 2 == 0, edge_recv[i, 0][1:2], edge_recv[i, 1][0:1]
        )
        high = both.astype(BF16).astype(F32)
        return jnp.where(r8w < 2, high, jnp.where(r8w < 4, both - high, 0.0)).astype(BF16)

    around = sides(1)
    above = dot_nt(jnp.where(l8w == r8w * 32 + 31, 1.0, 0.0).astype(BF16), sides(0))
    below = dot_nt(jnp.where(l8w == r8w * 32, 1.0, 0.0).astype(BF16), sides(2))
    above, below = above.astype(BF16), below.astype(BF16)
    ys, xs = iota((TY, 128), 0), iota((TX, 128), 0)

    def blend(near, far, at):
        return jnp.where(at == near, 0.75, 0.0) + jnp.where(at == far, 0.25, 0.0)

    val_copies = []
    for db in range(LON):
        spot = p_all[db * 8 : db * 8 + 1].astype(I32)
        i, j = spot >> 8, spot & 255
        nx, ny = i >> 1, j >> 1
        fx, fy = nx + 2 * (i & 1) - 1, ny + 2 * (j & 1) - 1
        cols = blend(ny, fy, ys).astype(BF16)
        side = jnp.where(
            r8 < 4, jnp.where(r8 % 2 == 0, blend(ny, fy, -1), blend(ny, fy, TY)), 0.0
        ).astype(BF16)
        inner = dot(wh, cols) + dot(wl, cols) + dot_tn(around, side)
        inner = jnp.sum(inner.reshape(8, TX, 128) * blend(nx, fx, xs)[None], axis=1)
        up = dot(top[0], cols) + dot(top[1], cols) + dot(above, side)
        down = dot(bottom[0], cols) + dot(bottom[1], cols) + dot(below, side)
        inner = inner + up * blend(nx, fx, -1) + down * blend(nx, fx, TX)
        val[db] = jnp.sum(inner * w_all[db * 8 : db * 8 + 8], axis=0, keepdims=True)
        for zo in range(ZH):
            n = zo * LON + db
            if n:
                copy = remote(
                    val.at[db], val_recv.at[n], val_s.at[n - 1], val_r.at[n - 1],
                    ((mem + zo * Y * C) % (ZH * Y * C), a, (b - db + LON) % LON),
                )
                copy.start()
                val_copies.append(copy)
    val_recv[0] = val[0]
    for copy in val_copies:
        copy.wait_recv()
    for db in range(LON):
        vsum[db : db + 1, :] = val_recv[db] + val_recv[LON + db]
    yc_copies = []
    for d in range(1, Y * C):
        copy = remote(
            vsum, yc_recv.at[d - 1], yc_s.at[d - 1], yc_r.at[d - 1],
            (zh * Y * C + (q + d) % (Y * C), a, b),
        )
        copy.start()
        yc_copies.append(copy)
    for copy in yc_copies:
        copy.wait_recv()
    mine = vsum[...]
    for d in range(Y * C - 1):
        mine = mine + yc_recv[d]
    vsum2[...] = mine
    x_copies = []
    for d in range(1, LAT):
        copy = remote(
            vsum2, x_recv.at[d - 1], x_s.at[d - 1], x_r.at[d - 1], (mem, (a + d) % LAT, b)
        )
        copy.start()
        x_copies.append(copy)
    for copy in x_copies:
        copy.wait_recv()
    table = jnp.concatenate([mine, x_recv[2], x_recv[1], x_recv[0]], 0)
    marks = marks.astype(BF16)
    found = sum(dot_tn(part, marks) for part in thirds(table))
    here = iota((128, 512), 0) == (rel >> 3) * 32 + rank
    equivalent = jnp.sum(jnp.where(here, found, 0.0), axis=0, keepdims=True)
    live = iota((1, 512), 1) < count[0]
    dep_ref[...] = jnp.where(live, innovation[...] - equivalent, 0.0)

    z_copy.wait_recv()
    inc_ref[...] = red2[pl.ds(zh * 4, 4)] + z_recv[...]
    for copy in (*lat_copies, *lon_copies, *pk_copies, core_copy, *y_copies, z_copy):
        copy.wait_send()
    for copy in (*val_copies, *yc_copies, *x_copies):
        copy.wait_send()
    for copy, sends, _ in halo:
        pl.when(sends)(copy.wait_send)


def per_device(
    perturbation, control, filter_length, modes, obs_weights, innovation, obs_tile,
    obs_column, obs_count,
):
    il = 1.0 / filter_length
    rate = jnp.exp(-il)
    gain = (1.0 - rate) / ((1.0 + rate) * math.sqrt(4 * ZH * Y * C - 1))
    vmem = pl.BlockSpec(memory_space=pltpu.VMEM)
    anywhere = pl.BlockSpec(memory_space=pl.ANY)
    smem = pl.BlockSpec(memory_space=pltpu.SMEM)
    f32 = lambda *shape: pltpu.VMEM(shape, F32)
    sem = lambda *shape: pltpu.SemaphoreType.DMA(shape)
    pairs = lambda *shape: [sem(*shape), sem(*shape)]
    increment, departures = pl.pallas_call(
        kernel,
        out_shape=(
            jax.ShapeDtypeStruct((4, TX, TY), F32),
            jax.ShapeDtypeStruct((1, 512), F32),
        ),
        in_specs=[vmem] * 7 + [smem] + [anywhere] * 2,
        out_specs=(vmem, vmem),
        scratch_shapes=[
            pltpu.VMEM((4, 16, TX, TY), BF16), pltpu.VMEM((4, 64, TX, TY), BF16),
            f32(16, 128, TY),
            f32(2, 4, 16, TY), f32(LAT - 1, 4, 16, TY),
            f32(2, 16, 128), f32(LON - 1, 16, 128),
            f32(TILES, 8, 128), f32(TILES, 8, 128),
            f32(8, 2, 4, TX, TY), f32(8, 4, TX, TY),
            f32(2, 4, 4, TX, TY), f32(Y - 1, 2, 4, TX, TY),
            f32(8, TX, TY), f32(4, TX, TY),
            f32(2, 8, 128), f32(2, 8, 128), f32(8, 256), f32(3, 2, 8, 256),
            f32(LON, 1, 128), f32(ZH * LON, 1, 128), f32(8, 128),
            f32(Y * C - 1, 8, 128), f32(8, 128), f32(LAT - 1, 8, 128),
            sem(2), *pairs(LAT - 1), *pairs(LON - 1), *pairs(TILES - 1), *pairs(1),
            *pairs(Y - 1), *pairs(1), *pairs(2), *pairs(3, 2), *pairs(ZH * LON - 1),
            *pairs(Y * C - 1), *pairs(LAT - 1),
        ],
        compiler_params=pltpu.CompilerParams(
            collective_id=0, has_side_effects=True, vmem_limit_bytes=48 * 2**20
        ),
        name="hybrid",
    )(
        jnp.broadcast_to(il[:, None], (16, 128)),
        jnp.broadcast_to(jnp.repeat(il, TX)[None], (8, 512)),
        modes * gain[None, :],
        obs_weights,
        innovation.reshape(1, 512),
        obs_tile.reshape(1, 512),
        obs_column.reshape(1, 512),
        obs_count,
        control,
        perturbation,
    )
    return increment, departures.reshape(512)


def solution(mesh):
    placed = (
        P("mem", None, "lat", "lon"),
        P("mem", None, "lat", "lon"),
        P(),
        P(),
        P(("lat", "lon"), None),
        P(("lat", "lon")),
        P(("lat", "lon"), None),
        P(("lat", "lon")),
        P(("lat", "lon")),
    )
    return jax.shard_map(
        per_device,
        mesh=mesh,
        in_specs=placed,
        out_specs=(P("mem", "lat", "lon"), P(("lat", "lon"))),
        check_vma=False,
    )
```

time: 318 us -> 70.3 us (0.22)
  local copies, waits for them, and re-layouts: 123 us -> 7.86 us
  starting transfers between devices: 97 us -> 0 us
  Pallas kernels: 0 us -> 60.1 us
  blocking collectives: 44.6 us -> 0 us
  waiting for transfers between devices: 28.2 us -> 0 us
  matrix products: 14 us -> 0 us
  other arithmetic: 6.94 us -> 0.67 us
    scatter x3 -> x0, local copies, waits for them, and re-layouts: 92.2 us -> none  [the longest x1 67.7 us: per_device(): column_send = jnp.zeros((tiles, capacity), jnp.float32).at[target, rankin...]
    all_to_all x7 -> x0, starting transfers between devices: 88.2 us -> none  [the longest x1 37 us: per_device(): lax.all_to_all(weight_send, ('lat', 'lon'), split_axis=0, concat_axis=0,...]
    pallas_call x0 -> x1, Pallas kernels: none -> 60.1 us  [per_device(): pl.pallas_call(kernel, out_shape=(jax.ShapeDtypeStruct((4, TX, TY), F32),...]
    all_to_all x2 -> x0, blocking collectives: 44.6 us -> none  [the longest x1 22.9 us: sent_to_all(): return lax.all_to_all(copies, axis, split_axis=0, concat_axis=0, tiled=True)]
    all_to_all x7 -> x0, waiting for transfers between devices: 22.4 us -> none  [the longest x4 18.1 us: sent_to_all(): return lax.all_to_all(copies, axis, split_axis=0, concat_axis=0, tiled=True)]
    gather x9 -> x0, local copies, waits for them, and re-layouts: 15.8 us -> none  [the longest x1 3.76 us: per_device(): equivalent = returned[target, ranking]]
    dot_general x5 -> x0, matrix products: 14 us -> none  [the longest x1 5.5 us: per_device(): profile = jnp.einsum('zk,mkp->mzp', modes, flat_field, precision=HIGH)]
    ppermute x4 -> x0, starting transfers between devices: 8.81 us -> none  [the longest x2 6.23 us: with_halo(): lax.ppermute(lax.slice_in_dim(block, block.shape[dim] - width, None, axis...]
  transfers between devices with their start and end apart: 11 -> 0, of which waited for: 7 -> 0; matrix products, arithmetic and copies ran while one was open for 35% -> 0% of each run, Pallas kernels for 0% -> 0%
where the time goes in v1:
time: 70.3 us; the launch traced here: 70 us
  Pallas kernels  60.1 us (85%)
  local copies, waits for them, and re-layouts  7.86 us (11%)
  between operations  1.31 us (2%)
    pallas_call x1, Pallas kernels, per_device(): pl.pallas_call(kernel, out_shape=(jax.ShapeDtypeStruct((4, TX, TY), F32),...  60.1 us
    unnamed x14, local copies, waits for them, and re-layouts  7.64 us

profile of v1, /device:TPU:1, one launch (start us, length us, event | category | flops | bytes accessed | tf_op | source)
XLA Modules:
  0.0 70.0 jit_solution(13612616391451756741)
XLA Ops:
  1.3 0.7 multiply_divide_fusion
  1.9 0.1 broadcast_in_dim.18
  2.0 0.1 broadcast_in_dim.19
  2.1 0.1 broadcast_in_dim.8.il_b
  2.2 0.8 %copy.13 = f32[64,16]{1,0:T(8,128)S(1)} copy(f32[64,16]{0,1:T(8,128)} %param.12) | data formatting | bytes 8192 | tf_op args[3]
  3.0 1.0 %copy.15.weights = bf16[512,64]{1,0:T(8,128)(2,1)S(1)} copy(bf16[512,64]{0,1:T(8,128)(2,1)} %param.13) | data formatting | bytes 131072 | tf_op args[4]
  3.9 0.0 copy-start
  3.9 1.6 %copy-done = bf16[4,64,32,128]{3,2,1,0:T(8,128)(2,1)S(1)} copy-done((bf16[4,64,32,128]{3,2,1,0:T(8,128)(2,1)S(1)}, bf16[4,64,32,128]{3,2,1,0:T(8,128)(2,1)}, u32[]{:S(2)}) %copy-start) | copy-done | bytes 2097176
  5.5 0.0 copy-start.1
  5.5 1.0 %copy-done.1 = bf16[4,16,32,128]{3,2,1,0:T(8,128)(2,1)S(1)} copy-done((bf16[4,16,32,128]{3,2,1,0:T(8,128)(2,1)S(1)}, bf16[4,16,32,128]{3,2,1,0:T(8,128)(2,1)}, u32[]{:S(2)}) %copy-start.1) | copy-done | bytes 524312
  6.6 0.0 copy-start.2
  6.6 0.7 copy-done.2
  7.3 0.0 copy-start.3
  7.3 0.7 copy-done.3
  7.9 0.0 copy-start.4
  7.9 0.7 copy-done.4
  8.6 60.1 %hybrid.1 = (f32[4,32,128]{2,1,0:T(8,128)S(1)}, f32[1,512]{1,0:T(1,128)S(1)}) custom-call(f32[16,128]{1,0:T(8,128)S(1)} %broadcast_in_dim.8.il_b, f32[8,512]{1,0:T(8,128)S(1)} %broadcast_in_dim.20.il_kx, f32[64,16]{1,0:T(8,128)S(1)} %broadcast_multiply_fusion.modes, bf16[512,64]{1,0:T(8,128)(2,1)S(1)} %copy.15.weights, f32[1,512]{1,0:T(1,128)S(1)} %bitcast.5, ...), custom_call_target="tpu_custom_call" | custom-call | tf_op jit(solution)/shard_map/hybrid/pallas_call | solution.py:417
  68.8 0.6 copy.19
  69.4 0.6 copy.20
  (2 shorter events, 0.0 us)
Async XLA Ops:
  3.9 1.6 %copy-start = (bf16[4,64,32,128]{3,2,1,0:T(8,128)(2,1)S(1)}, bf16[4,64,32,128]{3,2,1,0:T(8,128)(2,1)}, u32[]{:S(2)}) copy-start(bf16[4,64,32,128]{3,2,1,0:T(8,128)(2,1)} %pert_hbm.1) | copy-start | bytes 6291460
  5.5 1.0 %copy-start.1 = (bf16[4,16,32,128]{3,2,1,0:T(8,128)(2,1)S(1)}, bf16[4,16,32,128]{3,2,1,0:T(8,128)(2,1)}, u32[]{:S(2)}) copy-start(bf16[4,16,32,128]{3,2,1,0:T(8,128)(2,1)} %ctrl_hbm.1) | copy-start | bytes 1572868
  6.6 0.7 copy-start.2
  7.3 0.7 copy-start.3
  7.9 0.7 copy-start.4

commit v2 on v1

--- a/solution.py
+++ b/solution.py
@@ -42,8 +42,9 @@
 
 
 def kernel(
-    il_b, il_kx, modes, weights, innovation, tgt, col, count, ctrl_hbm, pert_hbm,
+    length_hbm, modes_hbm, weights_hbm, innovation_hbm, tgt_hbm, col_hbm, count, ctrl_hbm, pert_hbm,
     inc_ref, dep_ref,
+    length, modes, weights, innovation, tgt, col,
     ctrl, pert, field, lat_send, lat_recv, lon_send, lon_recv, pk_send, pk_recv,
     total, core_recv, red1, y_recv, red2, z_recv,
     row_send, row_recv, edge_send, edge_recv, val, val_recv, vsum, yc_recv, vsum2, x_recv,
@@ -59,10 +60,16 @@
             src_ref=src, dst_ref=dst, send_sem=s, recv_sem=r, device_id=dev, device_id_type=MESH
         )
 
-    load_c = pltpu.make_async_copy(ctrl_hbm, ctrl, load_sem.at[0])
-    load_p = pltpu.make_async_copy(pert_hbm, pert, load_sem.at[1])
-    load_c.start()
-    load_p.start()
+    loads = [
+        pltpu.make_async_copy(src, dst, load_sem.at[n])
+        for n, (src, dst) in enumerate((
+            (length_hbm, length), (ctrl_hbm, ctrl), (tgt_hbm, tgt), (col_hbm, col),
+            (weights_hbm, weights), (modes_hbm, modes), (innovation_hbm, innovation),
+            (pert_hbm, pert),
+        ))
+    ]
+    for load in loads:
+        load.start()
     row_recv[...] = jnp.zeros_like(row_recv)
     edge_recv[...] = jnp.zeros_like(edge_recv)
 
@@ -80,7 +87,13 @@
 
     rest_x = (NX - TX * a).astype(F32)
     rest_y = (NY - TY * b).astype(F32)
-    load_c.wait()
+    loads[0].wait()
+    ilc = jnp.where(iota((16, 16), 0) == iota((16, 16), 1), 1.0 / length[...], 0.0)
+    ilc = jnp.sum(ilc, axis=1, keepdims=True)
+    ilb = jnp.broadcast_to(ilc, (16, 128))
+    il_kx = jnp.where(iota((16, 512), 0) == iota((16, 512), 1) >> 5, ilc, 0.0)
+    il_kx = jnp.sum(il_kx, axis=0, keepdims=True)
+    loads[1].wait()
     for g in range(2):
         il = il_kx[0:1, g * 256 : (g + 1) * 256]
         rows, cols = iota((16, 256), 0), iota((16, 256), 1)
@@ -117,6 +130,8 @@
             out = dot(high, s) + dot(low, s)
             field[g * 8 : (g + 1) * 8, m * TX : (m + 1) * TX, :] = out.reshape(8, TX, TY)
 
+    for load in loads[2:5]:
+        load.wait()
     t = tgt[...]
     rel = (((t >> 3) + (LAT - a)) & 3) * LON + (((t & 7) + (LON - b)) & 7)
     marks = jnp.where(iota((TILES, 512), 0) == rel, 1.0, 0.0)
@@ -124,29 +139,29 @@
     rank = jnp.sum(dot(marks.astype(BF16), before) * marks, axis=0, keepdims=True).astype(I32)
     slot = rel * 32 + rank
     chosen = jnp.where(iota((1024, 512), 0) == slot, 1.0, 0.0).astype(BF16)
-    r8 = iota((8, 64), 0)
-    level = (r8 >> 2) * 32 + q * 4 + (r8 & 3)
-    own = jnp.where(iota((8, 64), 1) == level, 1.0, 0.0).astype(BF16)
-    picked = dot_nt(own, weights[...])
+    r32 = iota((32, 64), 0)
+    level = (r32 >> 2) * 8 + c * 4 + (r32 & 3)
+    own = jnp.where(iota((32, 64), 1) == level, 1.0, 0.0).astype(BF16)
+    picked = dot(own, weights[...])
     place = col[...]
     r8 = iota((8, 512), 0)
     places = jnp.where(r8 == 0, (place >> 7).astype(F32), (place & 127).astype(F32))
     packed = dot_nt(jnp.concatenate([picked, places], 0).astype(BF16), chosen)
-    spot = jnp.broadcast_to(packed[8:9] * 128.0 + packed[9:10], (8, 1024))
-    lane = iota((8, 128), 1)
+    spot = jnp.broadcast_to(packed[32:33] * 128.0 + packed[33:34], (8, 1024))
+    group = iota((8, 128), 1) >> 5
+
+    def turned(v, quarters):
+        return pltpu.roll(v, 32 * (quarters % 4), 1) if quarters % 4 else v
+
     for k in range(TILES):
         block, j = slice(k // 4 * 128, k // 4 * 128 + 128), k % 4
-        w = packed[0:8, block]
-        p = spot[:, block]
-        w = pltpu.roll(w, (128 - 32 * j) % 128, 1) if j else w
-        p = pltpu.roll(p, (160 - 32 * j) % 128, 1) if j != 1 else p
-        tile = jnp.where(lane < 32, w, p)
-        if k:
-            pk_send[k] = tile
-        else:
-            pk_recv[0] = tile
-
-    ilb = il_b[...]
+        tile = turned(packed[0:8, block], -j)
+        for g in range(1, 4):
+            tile = jnp.where(group == g, turned(packed[8 * g : 8 * g + 8, block], g - j), tile)
+        into = pk_send if k else pk_recv
+        into[k, 0:8, :] = tile
+        into[k, 8:9, :] = turned(spot[:, block], -j)[0:1]
+
     carry_l, carry_r = [0.0] * 4, [0.0] * 4
     for d in range(1, LAT):
         lat_copies[d - 1].wait_recv()
@@ -185,6 +200,15 @@
         copy.start()
         lon_copies.append(copy)
 
+    pk_copies = []
+    for k in range(1, TILES):
+        copy = remote(
+            pk_send.at[k], pk_recv.at[k], pk_s.at[k - 1], pk_r.at[k - 1],
+            (mem, (a + k // LON) % LAT, (b + k % LON) % LON),
+        )
+        copy.start()
+        pk_copies.append(copy)
+
     y1, y2 = iota((TY, TY), 0).astype(F32), iota((TY, TY), 1).astype(F32)
     for k in range(16):
         il = ilb[k : k + 1]
@@ -194,12 +218,17 @@
         fh, fl = halves(field[k])
         field[k] = dot(fh, nh) + dot(fl, nh) + dot(fh, nl)
 
+    loads[5].wait()
+    half = 0.5 * ilc
+    sq = half * half
+    gain = half * (1.0 - sq * (1.0 / 3.0 - sq * (2.0 / 15.0 - sq * (17.0 / 315.0))))
+    scaled = modes[...] * (gain * (1.0 / math.sqrt(4 * ZH * Y * C - 1)))
     spread = jnp.where(iota((512, 64), 0) >> 3 == iota((512, 64), 1), 1.0, 0.0).astype(BF16)
     widen = jnp.where(iota((16, 128), 0) == iota((16, 128), 1) >> 3, 1.0, 0.0).astype(BF16)
     diagonal = (iota((512, 128), 0) & 7) == (iota((512, 128), 1) & 7)
     mh, ml = (
-        jnp.where(diagonal, dot(dot(spread, part).astype(BF16), widen), 0.0).astype(BF16)
-        for part in halves(modes[...])
+        jnp.where(diagonal, dot(spread, dot_tn(part, widen).astype(BF16)), 0.0).astype(BF16)
+        for part in halves(scaled)
     )
 
     cl, cr = 0.0, 0.0
@@ -209,14 +238,6 @@
         got = lon_recv[d - 1]
         cl = cl + (jnp.exp(-128.0 * (d - 1) * ilb) * left) * got
         cr = cr + (jnp.exp(-128.0 * (LON - 1 - d) * ilb) * (1.0 - left)) * got
-    pk_copies = []
-    for k in range(1, TILES):
-        copy = remote(
-            pk_send.at[k], pk_recv.at[k], pk_s.at[k - 1], pk_r.at[k - 1],
-            (mem, (a + k // LON) % LAT, (b + k % LON) % LON),
-        )
-        copy.start()
-        pk_copies.append(copy)
     for k in range(16):
         il = ilb[k : k + 1]
         ahead = jnp.exp(-(ly + 1.0) * il) - jnp.exp((ly - 1.0 - 2.0 * rest_y) * il)
@@ -227,7 +248,8 @@
         )
         field[k] = field[k] + (dot_tn(ch, ah) + dot_tn(co, ah) + dot_tn(ch, al))
 
-    load_p.wait()
+    loads[7].wait()
+    core_copies = []
     for xb in range(4):
         acc = None
         for m in range(4):
@@ -237,13 +259,18 @@
             p = pert[m, :, xb * 8 : xb * 8 + 8, :].astype(F32).reshape(512, 128)
             acc = prof * p if acc is None else acc + prof * p
         total[:, :, :, xb * 8 : xb * 8 + 8, :] = acc.reshape(8, 2, 4, 8, 128)
-
-    core_copy = remote(
-        total.at[:, 1 - c], core_recv, core_s.at[0], core_r.at[0], (mem + 1 - 2 * c, a, b)
-    )
-    core_copy.start()
-    core_copy.wait_recv()
-    red1[...] = (total[:, c] + core_recv[...]).reshape(2, 4, 4, TX, TY)
+        part = pl.ds(xb * 8, 8)
+        copy = remote(
+            total.at[:, 1 - c, :, part, :], core_recv.at[:, :, part, :],
+            core_s.at[xb], core_r.at[xb], (mem + 1 - 2 * c, a, b),
+        )
+        copy.start()
+        core_copies.append(copy)
+
+    for copy in core_copies:
+        copy.wait_recv()
+    whole = total[:, c] + core_recv[...]
+    red1[...] = whole.reshape(2, 4, 4, TX, TY)
     y_copies = []
     for d in range(1, Y):
         yp = (y + d) % Y
@@ -254,35 +281,15 @@
         copy.start()
         y_copies.append(copy)
 
-    w_all, p_all = jnp.zeros((64, 128), F32), jnp.zeros((64, 128), F32)
-    group = iota((64, 128), 1) >> 5
-    for da in range(LAT):
-        for k in range(max(1, da * LON), (da + 1) * LON):
-            pk_copies[k - 1].wait_recv()
-        got = pk_recv[da * LON : (da + 1) * LON].reshape(64, 128)
-        w = pltpu.roll(got, 32 * da, 1) if da else got
-        p = pltpu.roll(got, (32 * da + 96) % 128, 1) if da != 1 else got
-        w_all = jnp.where(group == da, w, w_all)
-        p_all = jnp.where(group == da, p, p_all)
-
-    for copy in y_copies:
-        copy.wait_recv()
-    whole = red1[:, y] + y_recv[0] + y_recv[1] + y_recv[2]
-    whole = whole.reshape(8, TX, TY)
-    red2[...] = whole
-    z_copy = remote(
-        red2.at[pl.ds((1 - zh) * 4, 4)], z_recv, z_s.at[0], z_r.at[0],
-        ((mem + Y * C) % (ZH * Y * C), a, b),
-    )
-
+    lane = iota((8, 128), 1)
     r8 = iota((8, 128), 0)
     ends = jnp.where(
         (r8 == 0) & (lane == 0) | (r8 == 1) & (lane == 127), 1.0, 0.0
     ).astype(BF16)
-    wh, wl = halves(whole.reshape(256, 128))
-    row_send[0] = red2[:, TX - 1, :]
-    row_send[1] = red2[:, 0, :]
-    edge_send[...] = dot_nt(ends, wh) + dot_nt(ends, wl)
+    wh, wl = halves(whole.reshape(1024, 128))
+    row_send[0] = red1[:, :, :, TX - 1, :].reshape(32, 128)
+    row_send[1] = red1[:, :, :, 0, :].reshape(32, 128)
+    edge_send[...] = (dot_nt(ends, wh) + dot_nt(ends, wl))[0:2]
     halo = []
     for s in range(2):
         step = 1 - 2 * s
@@ -306,46 +313,68 @@
             ))
     for copy, sends, _ in halo:
         pl.when(sends)(copy.start)
-    z_copy.start()
-    for copy, _, gets in halo:
-        pl.when(gets)(copy.wait_recv)
-
-    top, bottom = halves(row_recv[0]), halves(row_recv[1])
-    r8w = iota((8, 256), 0)
-    l8w = iota((8, 256), 1)
-
-    def sides(i):
-        both = jnp.where(
-            r8w % 2 == 0, edge_recv[i, 0][1:2], edge_recv[i, 1][0:1]
-        )
-        high = both.astype(BF16).astype(F32)
-        return jnp.where(r8w < 2, high, jnp.where(r8w < 4, both - high, 0.0)).astype(BF16)
-
-    around = sides(1)
-    above = dot_nt(jnp.where(l8w == r8w * 32 + 31, 1.0, 0.0).astype(BF16), sides(0))
-    below = dot_nt(jnp.where(l8w == r8w * 32, 1.0, 0.0).astype(BF16), sides(2))
-    above, below = above.astype(BF16), below.astype(BF16)
+
+    w_all, p_all = [jnp.zeros((64, 128), F32)] * 4, jnp.zeros((8, 128), F32)
+    g64 = iota((64, 128), 1) >> 5
+    for da in range(LAT):
+        for k in range(max(1, da * LON), (da + 1) * LON):
+            pk_copies[k - 1].wait_recv()
+        got = pk_recv[da * LON : (da + 1) * LON, 0:8, :].reshape(64, 128)
+        w_all = [
+            jnp.where(g64 == da, turned(got, da - g), w) for g, w in enumerate(w_all)
+        ]
+        p_all = jnp.where(
+            group == da, turned(pk_recv[da * LON : (da + 1) * LON, 8, :], da), p_all
+        )
     ys, xs = iota((TY, 128), 0), iota((TX, 128), 0)
 
     def blend(near, far, at):
         return jnp.where(at == near, 0.75, 0.0) + jnp.where(at == far, 0.25, 0.0)
 
-    val_copies = []
+    double = jnp.concatenate([wh, wl], 1)
+    spots = []
     for db in range(LON):
-        spot = p_all[db * 8 : db * 8 + 1].astype(I32)
+        spot = p_all[db : db + 1].astype(I32)
         i, j = spot >> 8, spot & 255
         nx, ny = i >> 1, j >> 1
         fx, fy = nx + 2 * (i & 1) - 1, ny + 2 * (j & 1) - 1
-        cols = blend(ny, fy, ys).astype(BF16)
-        side = jnp.where(
-            r8 < 4, jnp.where(r8 % 2 == 0, blend(ny, fy, -1), blend(ny, fy, TY)), 0.0
-        ).astype(BF16)
-        inner = dot(wh, cols) + dot(wl, cols) + dot_tn(around, side)
-        inner = jnp.sum(inner.reshape(8, TX, 128) * blend(nx, fx, xs)[None], axis=1)
-        up = dot(top[0], cols) + dot(top[1], cols) + dot(above, side)
-        down = dot(bottom[0], cols) + dot(bottom[1], cols) + dot(below, side)
-        inner = inner + up * blend(nx, fx, -1) + down * blend(nx, fx, TX)
-        val[db] = jnp.sum(inner * w_all[db * 8 : db * 8 + 8], axis=0, keepdims=True)
+        cols, rows = blend(ny, fy, ys).astype(BF16), blend(nx, fx, xs)
+        inner = dot(double, jnp.concatenate([cols, cols], 0))
+        inner = jnp.sum(inner.reshape(32, TX, 128) * rows[None], axis=1)
+        around = [blend(ny, fy, -1), blend(ny, fy, TY), blend(nx, fx, -1), blend(nx, fx, TX)]
+        spots.append((inner, cols, rows.astype(BF16), *around))
+
+    for copy, _, gets in halo:
+        pl.when(gets)(copy.wait_recv)
+    beyond = jnp.concatenate([*halves(row_recv[0]), *halves(row_recv[1])], 0)
+    z32, l32 = iota((32, 1024), 0), iota((32, 1024), 1)
+    fold = jnp.where(iota((1024, TX), 0) & 31 == iota((1024, TX), 1), 1.0, 0.0).astype(BF16)
+
+    def at_level(line, where):
+        return jnp.where(where, line, 0.0)
+
+    left, right = edge_recv[1, 0][1:2], edge_recv[1, 1][0:1]
+    same = l32 >> 5 == z32
+    beside = jnp.concatenate(
+        [*halves(at_level(left, same)), *halves(at_level(right, same))], 0
+    )
+    beside = dot(beside, fold).astype(BF16)
+    corner = [
+        jnp.sum(at_level(edge_recv[i, j][1 - j : 2 - j], l32 == z32 * 32 + x), 1, keepdims=True)
+        for i, x in ((0, TX - 1), (2, 0))
+        for j in range(2)
+    ]
+    val_copies = []
+    for db in range(LON):
+        inner, cols, rows, west, east, north, south = spots[db]
+        ud = dot(beyond, cols)
+        lr = dot(beside, rows)
+        up = ud[0:32] + ud[32:64] + corner[0] * west + corner[1] * east
+        down = ud[64:96] + ud[96:128] + corner[2] * west + corner[3] * east
+        inner = inner + (lr[0:32] + lr[32:64]) * west + (lr[64:96] + lr[96:128]) * east
+        inner = inner + up * north + down * south
+        w = jnp.concatenate([w[db * 8 : db * 8 + 8] for w in w_all], 0)
+        val[db] = jnp.sum(inner * w, axis=0, keepdims=True)
         for zo in range(ZH):
             n = zo * LON + db
             if n:
@@ -355,6 +384,16 @@
                 )
                 copy.start()
                 val_copies.append(copy)
+
+    for copy in y_copies:
+        copy.wait_recv()
+    red2[...] = red1[:, y] + y_recv[0] + y_recv[1] + y_recv[2]
+    z_copy = remote(
+        red2.at[1 - zh], z_recv, z_s.at[0], z_r.at[0],
+        ((mem + Y * C) % (ZH * Y * C), a, b),
+    )
+    z_copy.start()
+
     val_recv[0] = val[0]
     for copy in val_copies:
         copy.wait_recv()
@@ -388,12 +427,13 @@
     found = sum(dot_tn(part, marks) for part in thirds(table))
     here = iota((128, 512), 0) == (rel >> 3) * 32 + rank
     equivalent = jnp.sum(jnp.where(here, found, 0.0), axis=0, keepdims=True)
+    loads[6].wait()
     live = iota((1, 512), 1) < count[0]
     dep_ref[...] = jnp.where(live, innovation[...] - equivalent, 0.0)
 
     z_copy.wait_recv()
-    inc_ref[...] = red2[pl.ds(zh * 4, 4)] + z_recv[...]
-    for copy in (*lat_copies, *lon_copies, *pk_copies, core_copy, *y_copies, z_copy):
+    inc_ref[...] = red2[zh] + z_recv[...]
+    for copy in (*lat_copies, *lon_copies, *pk_copies, *core_copies, *y_copies, z_copy):
         copy.wait_send()
     for copy in (*val_copies, *yc_copies, *x_copies):
         copy.wait_send()
@@ -405,11 +445,8 @@
     perturbation, control, filter_length, modes, obs_weights, innovation, obs_tile,
     obs_column, obs_count,
 ):
-    il = 1.0 / filter_length
-    rate = jnp.exp(-il)
-    gain = (1.0 - rate) / ((1.0 + rate) * math.sqrt(4 * ZH * Y * C - 1))
     vmem = pl.BlockSpec(memory_space=pltpu.VMEM)
-    anywhere = pl.BlockSpec(memory_space=pl.ANY)
+    hbm = pl.BlockSpec(memory_space=pltpu.HBM)
     smem = pl.BlockSpec(memory_space=pltpu.SMEM)
     f32 = lambda *shape: pltpu.VMEM(shape, F32)
     sem = lambda *shape: pltpu.SemaphoreType.DMA(shape)
@@ -420,33 +457,34 @@
             jax.ShapeDtypeStruct((4, TX, TY), F32),
             jax.ShapeDtypeStruct((1, 512), F32),
         ),
-        in_specs=[vmem] * 7 + [smem] + [anywhere] * 2,
+        in_specs=[hbm] * 6 + [smem] + [hbm] * 2,
         out_specs=(vmem, vmem),
         scratch_shapes=[
+            f32(1, 16), f32(16, 64), pltpu.VMEM((64, 512), BF16), f32(1, 512),
+            pltpu.VMEM((1, 512), I32), pltpu.VMEM((1, 512), I32),
             pltpu.VMEM((4, 16, TX, TY), BF16), pltpu.VMEM((4, 64, TX, TY), BF16),
             f32(16, 128, TY),
             f32(2, 4, 16, TY), f32(LAT - 1, 4, 16, TY),
             f32(2, 16, 128), f32(LON - 1, 16, 128),
-            f32(TILES, 8, 128), f32(TILES, 8, 128),
+            f32(TILES, 9, 128), f32(TILES, 9, 128),
             f32(8, 2, 4, TX, TY), f32(8, 4, TX, TY),
             f32(2, 4, 4, TX, TY), f32(Y - 1, 2, 4, TX, TY),
-            f32(8, TX, TY), f32(4, TX, TY),
-            f32(2, 8, 128), f32(2, 8, 128), f32(8, 256), f32(3, 2, 8, 256),
+            f32(2, 4, TX, TY), f32(4, TX, TY),
+            f32(2, 32, 128), f32(2, 32, 128), f32(2, 1024), f32(3, 2, 2, 1024),
             f32(LON, 1, 128), f32(ZH * LON, 1, 128), f32(8, 128),
             f32(Y * C - 1, 8, 128), f32(8, 128), f32(LAT - 1, 8, 128),
-            sem(2), *pairs(LAT - 1), *pairs(LON - 1), *pairs(TILES - 1), *pairs(1),
+            sem(8), *pairs(LAT - 1), *pairs(LON - 1), *pairs(TILES - 1), *pairs(4),
             *pairs(Y - 1), *pairs(1), *pairs(2), *pairs(3, 2), *pairs(ZH * LON - 1),
             *pairs(Y * C - 1), *pairs(LAT - 1),
         ],
         compiler_params=pltpu.CompilerParams(
-            collective_id=0, has_side_effects=True, vmem_limit_bytes=48 * 2**20
+            collective_id=0, has_side_effects=True, vmem_limit_bytes=60_000_000
         ),
         name="hybrid",
     )(
-        jnp.broadcast_to(il[:, None], (16, 128)),
-        jnp.broadcast_to(jnp.repeat(il, TX)[None], (8, 512)),
-        modes * gain[None, :],
-        obs_weights,
+        filter_length.reshape(1, 16),
+        modes.T,
+        obs_weights.T,
         innovation.reshape(1, 512),
         obs_tile.reshape(1, 512),
         obs_column.reshape(1, 512),

time: 70.3 us -> 58.5 us (0.83)
  Pallas kernels: 60.1 us -> 54.2 us
  local copies, waits for them, and re-layouts: 7.86 us -> 2.72 us
    pallas_call x1, Pallas kernels: 60.1 us -> 54.2 us  [per_device(): pl.pallas_call(kernel, out_shape=(jax.ShapeDtypeStruct((4, TX, TY), F32),...]
    unnamed x14 -> x2, local copies, waits for them, and re-layouts: 7.64 us -> 2.72 us
where the time goes in v2:
time: 58.5 us; the launch traced here: 58.3 us
  Pallas kernels  54.2 us (93%)
  local copies, waits for them, and re-layouts  2.72 us (5%)
  between operations  1.29 us (2%)
    pallas_call x1, Pallas kernels, per_device(): pl.pallas_call(kernel, out_shape=(jax.ShapeDtypeStruct((4, TX, TY), F32),...  54.2 us
    unnamed x2, local copies, waits for them, and re-layouts  2.72 us

profile of v2, /device:TPU:1, one launch (start us, length us, event | category | flops | bytes accessed | tf_op | source)
XLA Modules:
  0.0 58.3 jit_solution(10152785029601257024)
XLA Ops:
  1.3 54.2 %hybrid.1 = (f32[4,32,128]{2,1,0:T(8,128)}, f32[1,512]{1,0:T(1,128)}) custom-call(f32[1,16]{1,0:T(1,128)} %bitcast.13, f32[16,64]{1,0:T(8,128)} %bitcast.8, bf16[64,512]{1,0:T(8,128)(2,1)} %bitcast.7, f32[1,512]{1,0:T(1,128)} %bitcast.10, s32[1,512]{1,0:T(1,128)} %bitcast.11, s32[1,512]{1,0:T(1,128)} %bitcast.12, s32[1]{0:T(128)S(6)} %copy.13.count, ...), custom_call_target="tpu_custom_call" | custom-call | tf_op jit(solution)/shard_map/hybrid/pallas_call | solution.py:454
  55.5 1.5 %copy.14 = f32[4,32,128]{2,1,0:T(8,128)} copy(f32[4,32,128]{2,1,0:T(8,128)} %get-tuple-element.8) | data formatting | bytes 131072
  57.0 1.2 %copy.15 = f32[512]{0:T(512)} copy(f32[512]{0:T(512)} %bitcast.9) | data formatting | bytes 4096

commit v3 on v2

--- a/solution.py
+++ b/solution.py
@@ -43,13 +43,13 @@
 
 def kernel(
     length_hbm, modes_hbm, weights_hbm, innovation_hbm, tgt_hbm, col_hbm, count, ctrl_hbm, pert_hbm,
-    inc_ref, dep_ref,
+    inc_hbm, dep_hbm,
     length, modes, weights, innovation, tgt, col,
     ctrl, pert, field, lat_send, lat_recv, lon_send, lon_recv, pk_send, pk_recv,
     total, core_recv, red1, y_recv, red2, z_recv,
-    row_send, row_recv, edge_send, edge_recv, val, val_recv, vsum, yc_recv, vsum2, x_recv,
+    row_send, row_recv, edge_send, edge_recv, val, val_recv, vsum, last_send, last_recv, inc_ref, dep_ref,
     load_sem, lat_s, lat_r, lon_s, lon_r, pk_s, pk_r, core_s, core_r, y_s, y_r, z_s, z_r,
-    row_s, row_r, edge_s, edge_r, val_s, val_r, yc_s, yc_r, x_s, x_r,
+    row_s, row_r, edge_s, edge_r, val_s, val_r, last_s, last_r,
 ):
     mem, a, b = (lax.axis_index(n) for n in ("mem", "lat", "lon"))
     zh, y, c = mem // (Y * C), (mem // C) % Y, mem % C
@@ -84,6 +84,9 @@
         greet((zh * Y * C + (q + d) % (Y * C), a, b))
     for d in range(LON):
         greet(((mem + Y * C) % (ZH * Y * C), a, (b + d) % LON))
+    for da in range(1, LAT):
+        for d in range(1, Y * C):
+            greet((zh * Y * C + (q + d) % (Y * C), (a + da) % LAT, b))
 
     rest_x = (NX - TX * a).astype(F32)
     rest_y = (NY - TY * b).astype(F32)
@@ -108,7 +111,7 @@
             lat_send[0, m, g * 8 : (g + 1) * 8, :] = e[0:8]
             lat_send[1, m, g * 8 : (g + 1) * 8, :] = e[8:16]
 
-    pl.semaphore_wait(barrier, TILES - 1 + Y * C - 1 + LON)
+    pl.semaphore_wait(barrier, TILES - 1 + LAT * (Y * C - 1) + LON)
     lat_copies = []
     for d in range(1, LAT):
         copy = remote(
@@ -129,6 +132,44 @@
             s = ctrl[m, g * 8 : (g + 1) * 8].reshape(256, 128)
             out = dot(high, s) + dot(low, s)
             field[g * 8 : (g + 1) * 8, m * TX : (m + 1) * TX, :] = out.reshape(8, TX, TY)
+
+    carry_l, carry_r = [0.0] * 4, [0.0] * 4
+    for d in range(1, LAT):
+        lat_copies[d - 1].wait_recv()
+        left = jnp.where(a >= d, 1.0, 0.0)
+        wl = jnp.exp(-32.0 * (d - 1) * ilb) * left
+        wr = jnp.exp(-32.0 * (LAT - 1 - d) * ilb) * (1.0 - left)
+        for m in range(4):
+            got = lat_recv[d - 1, m]
+            carry_l[m] = carry_l[m] + wl * got
+            carry_r[m] = carry_r[m] + wr * got
+    x = iota((TX, TY), 0).astype(F32)
+    ly = iota((8, TY), 1).astype(F32)
+    row8 = iota((8, TY), 0)
+    for k in range(16):
+        il = ilb[k : k + 1]
+        ahead = jnp.exp(-(x + 1.0) * il) - jnp.exp((x - 1.0 - 2.0 * rest_x) * il)
+        behind = jnp.exp((x - 32.0) * il)
+        for m in range(4):
+            here = slice(m * TX, (m + 1) * TX)
+            field[k, here, :] = (
+                field[k, here, :] + ahead * carry_l[m][k : k + 1] + behind * carry_r[m][k : k + 1]
+            )
+        up = jnp.exp((ly - 127.0) * il)
+        down = jnp.exp(-ly * il) - jnp.exp((ly - 2.0 * rest_y) * il)
+        th, tl = halves(jnp.where(row8 == 0, up, down))
+        fh, fl = halves(field[k])
+        e = dot_nt(th, fh) + dot_nt(th, fl) + dot_nt(tl, fh)
+        lon_send[0, k : k + 1, :] = e[0:1]
+        lon_send[1, k : k + 1, :] = e[1:2]
+    lon_copies = []
+    for d in range(1, LON):
+        copy = remote(
+            lon_send.at[(b + d) // LON], lon_recv.at[d - 1], lon_s.at[d - 1], lon_r.at[d - 1],
+            (mem, a, (b + d) % LON),
+        )
+        copy.start()
+        lon_copies.append(copy)
 
     for load in loads[2:5]:
         load.wait()
@@ -162,44 +203,6 @@
         into[k, 0:8, :] = tile
         into[k, 8:9, :] = turned(spot[:, block], -j)[0:1]
 
-    carry_l, carry_r = [0.0] * 4, [0.0] * 4
-    for d in range(1, LAT):
-        lat_copies[d - 1].wait_recv()
-        left = jnp.where(a >= d, 1.0, 0.0)
-        wl = jnp.exp(-32.0 * (d - 1) * ilb) * left
-        wr = jnp.exp(-32.0 * (LAT - 1 - d) * ilb) * (1.0 - left)
-        for m in range(4):
-            got = lat_recv[d - 1, m]
-            carry_l[m] = carry_l[m] + wl * got
-            carry_r[m] = carry_r[m] + wr * got
-    x = iota((TX, TY), 0).astype(F32)
-    ly = iota((8, TY), 1).astype(F32)
-    r8 = iota((8, TY), 0)
-    for k in range(16):
-        il = ilb[k : k + 1]
-        ahead = jnp.exp(-(x + 1.0) * il) - jnp.exp((x - 1.0 - 2.0 * rest_x) * il)
-        behind = jnp.exp((x - 32.0) * il)
-        for m in range(4):
-            here = slice(m * TX, (m + 1) * TX)
-            field[k, here, :] = (
-                field[k, here, :] + ahead * carry_l[m][k : k + 1] + behind * carry_r[m][k : k + 1]
-            )
-        up = jnp.exp((ly - 127.0) * il)
-        down = jnp.exp(-ly * il) - jnp.exp((ly - 2.0 * rest_y) * il)
-        th, tl = halves(jnp.where(r8 == 0, up, down))
-        fh, fl = halves(field[k])
-        e = dot_nt(th, fh) + dot_nt(th, fl) + dot_nt(tl, fh)
-        lon_send[0, k : k + 1, :] = e[0:1]
-        lon_send[1, k : k + 1, :] = e[1:2]
-    lon_copies = []
-    for d in range(1, LON):
-        copy = remote(
-            lon_send.at[(b + d) // LON], lon_recv.at[d - 1], lon_s.at[d - 1], lon_r.at[d - 1],
-            (mem, a, (b + d) % LON),
-        )
-        copy.start()
-        lon_copies.append(copy)
-
     pk_copies = []
     for k in range(1, TILES):
         copy = remote(
@@ -231,6 +234,8 @@
         for part in halves(scaled)
     )
 
+    mhh = jnp.concatenate([mh, mh], 1)
+
     cl, cr = 0.0, 0.0
     for d in range(1, LON):
         lon_copies[d - 1].wait_recv()
@@ -242,9 +247,9 @@
         il = ilb[k : k + 1]
         ahead = jnp.exp(-(ly + 1.0) * il) - jnp.exp((ly - 1.0 - 2.0 * rest_y) * il)
         behind = jnp.exp((ly - 128.0) * il)
-        ah, al = halves(jnp.where(r8 == 0, ahead, jnp.where(r8 == 1, behind, 0.0)))
+        ah, al = halves(jnp.where(row8 == 0, ahead, jnp.where(row8 == 1, behind, 0.0)))
         ch, co = halves(
-            jnp.where(r8 == 0, cl[k : k + 1], jnp.where(r8 == 1, cr[k : k + 1], 0.0))
+            jnp.where(row8 == 0, cl[k : k + 1], jnp.where(row8 == 1, cr[k : k + 1], 0.0))
         )
         field[k] = field[k] + (dot_tn(ch, ah) + dot_tn(co, ah) + dot_tn(ch, al))
 
@@ -252,12 +257,20 @@
     core_copies = []
     for xb in range(4):
         acc = None
-        for m in range(4):
-            rows = field[:, m * TX + xb * 8 : m * TX + xb * 8 + 8, :].reshape(128, 128)
+        for pair in range(2):
+            rows = jnp.concatenate(
+                [
+                    field[:, m * TX + xb * 8 : m * TX + xb * 8 + 8, :].reshape(128, 128)
+                    for m in (2 * pair, 2 * pair + 1)
+                ],
+                1,
+            )
             fh, fl = halves(rows)
-            prof = dot(mh, fh) + dot(mh, fl) + dot(ml, fh)
-            p = pert[m, :, xb * 8 : xb * 8 + 8, :].astype(F32).reshape(512, 128)
-            acc = prof * p if acc is None else acc + prof * p
+            prof = dot(mhh, jnp.concatenate([fh, fl], 0)) + dot(ml, fh)
+            for n in range(2):
+                p = pert[2 * pair + n, :, xb * 8 : xb * 8 + 8, :].astype(F32).reshape(512, 128)
+                term = prof[:, n * 128 : n * 128 + 128] * p
+                acc = term if acc is None else acc + term
         total[:, :, :, xb * 8 : xb * 8 + 8, :] = acc.reshape(8, 2, 4, 8, 128)
         part = pl.ds(xb * 8, 8)
         copy = remote(
@@ -272,14 +285,16 @@
     whole = total[:, c] + core_recv[...]
     red1[...] = whole.reshape(2, 4, 4, TX, TY)
     y_copies = []
-    for d in range(1, Y):
-        yp = (y + d) % Y
-        copy = remote(
-            red1.at[:, yp], y_recv.at[d - 1], y_s.at[d - 1], y_r.at[d - 1],
-            ((zh * Y + yp) * C + c, a, b),
-        )
-        copy.start()
-        y_copies.append(copy)
+    for h, half in enumerate((1 - zh, zh)):
+        for d in range(1, Y):
+            yp = (y + d) % Y
+            n = h * (Y - 1) + d - 1
+            copy = remote(
+                red1.at[half, yp], y_recv.at[n], y_s.at[n], y_r.at[n],
+                ((zh * Y + yp) * C + c, a, b),
+            )
+            copy.start()
+            y_copies.append(copy)
 
     lane = iota((8, 128), 1)
     r8 = iota((8, 128), 0)
@@ -385,11 +400,11 @@
                 copy.start()
                 val_copies.append(copy)
 
-    for copy in y_copies:
+    for copy in y_copies[: Y - 1]:
         copy.wait_recv()
-    red2[...] = red1[:, y] + y_recv[0] + y_recv[1] + y_recv[2]
+    red2[...] = red1[1 - zh, y] + y_recv[0] + y_recv[1] + y_recv[2]
     z_copy = remote(
-        red2.at[1 - zh], z_recv, z_s.at[0], z_r.at[0],
+        red2, z_recv, z_s.at[0], z_r.at[0],
         ((mem + Y * C) % (ZH * Y * C), a, b),
     )
     z_copy.start()
@@ -399,46 +414,77 @@
         copy.wait_recv()
     for db in range(LON):
         vsum[db : db + 1, :] = val_recv[db] + val_recv[LON + db]
-    yc_copies = []
-    for d in range(1, Y * C):
-        copy = remote(
-            vsum, yc_recv.at[d - 1], yc_s.at[d - 1], yc_r.at[d - 1],
-            (zh * Y * C + (q + d) % (Y * C), a, b),
-        )
-        copy.start()
-        yc_copies.append(copy)
-    for copy in yc_copies:
+    both = vsum[...]
+    kept = group == (iota((8, 128), 0) & 3)
+    for da in range(LAT):
+        mine = jnp.zeros((8, 128), F32)
+        for g in range(4):
+            mine = jnp.where(kept & (group == g), turned(both, g - da), mine)
+        mine = jnp.sum(mine.reshape(2, 4, 128), axis=1)
+        if da:
+            last_send[da - 1] = mine
+        else:
+            last_send[LAT - 1] = mine
+            last_recv[0] = mine
+    last_copies = []
+    for da in range(LAT):
+        for d in range(Y * C):
+            n = da * Y * C + d
+            if n:
+                copy = remote(
+                    last_send.at[(da + LAT - 1) % LAT], last_recv.at[n],
+                    last_s.at[n - 1], last_r.at[n - 1],
+                    (zh * Y * C + (q + d) % (Y * C), (a + LAT - da) % LAT, b),
+                )
+                copy.start()
+                last_copies.append(copy)
+    for copy in y_copies[Y - 1 :]:
         copy.wait_recv()
-    mine = vsum[...]
-    for d in range(Y * C - 1):
-        mine = mine + yc_recv[d]
-    vsum2[...] = mine
-    x_copies = []
-    for d in range(1, LAT):
-        copy = remote(
-            vsum2, x_recv.at[d - 1], x_s.at[d - 1], x_r.at[d - 1], (mem, (a + d) % LAT, b)
-        )
-        copy.start()
-        x_copies.append(copy)
-    for copy in x_copies:
+    own = red1[zh, y] + y_recv[3] + y_recv[4] + y_recv[5]
+    z_copy.wait_recv()
+    inc_ref[...] = own + z_recv[...]
+    inc_copy = pltpu.make_async_copy(inc_ref, inc_hbm, load_sem.at[9])
+    inc_copy.start()
+    for copy in last_copies:
         copy.wait_recv()
-    table = jnp.concatenate([mine, x_recv[2], x_recv[1], x_recv[0]], 0)
-    marks = marks.astype(BF16)
+    table = []
+    for da in range(LAT):
+        block = last_recv[da * Y * C]
+        for d in range(1, Y * C):
+            block = block + last_recv[da * Y * C + d]
+        table.append(block)
+    table = jnp.concatenate(table, 0)
+    marks = jnp.where(iota((8, 512), 0) == rel >> 2, 1.0, 0.0).astype(BF16)
     found = sum(dot_tn(part, marks) for part in thirds(table))
-    here = iota((128, 512), 0) == (rel >> 3) * 32 + rank
+    here = iota((128, 512), 0) == (rel & 3) * 32 + rank
     equivalent = jnp.sum(jnp.where(here, found, 0.0), axis=0, keepdims=True)
     loads[6].wait()
     live = iota((1, 512), 1) < count[0]
     dep_ref[...] = jnp.where(live, innovation[...] - equivalent, 0.0)
-
-    z_copy.wait_recv()
-    inc_ref[...] = red2[zh] + z_recv[...]
+    dep_copy = pltpu.make_async_copy(dep_ref, dep_hbm, load_sem.at[8])
+    dep_copy.start()
+    inc_copy.wait()
+    dep_copy.wait()
+
     for copy in (*lat_copies, *lon_copies, *pk_copies, *core_copies, *y_copies, z_copy):
         copy.wait_send()
-    for copy in (*val_copies, *yc_copies, *x_copies):
+    for copy in (*val_copies, *last_copies):
         copy.wait_send()
     for copy, sends, _ in halo:
         pl.when(sends)(copy.wait_send)
+
+
+def deliver(increment, departures, inc_hbm, dep_hbm, inc, dep, sems):
+    pairs = ((increment, inc, inc_hbm), (departures, dep, dep_hbm))
+    inward = [pltpu.make_async_copy(p[0], p[1], sems.at[n]) for n, p in enumerate(pairs)]
+    outward = [pltpu.make_async_copy(p[1], p[2], sems.at[2 + n]) for n, p in enumerate(pairs)]
+    for copy in inward:
+        copy.start()
+    for back, forth in zip(inward, outward):
+        back.wait()
+        forth.start()
+    for copy in outward:
+        copy.wait()
 
 
 def per_device(
@@ -458,7 +504,7 @@
             jax.ShapeDtypeStruct((1, 512), F32),
         ),
         in_specs=[hbm] * 6 + [smem] + [hbm] * 2,
-        out_specs=(vmem, vmem),
+        out_specs=(hbm, hbm),
         scratch_shapes=[
             f32(1, 16), f32(16, 64), pltpu.VMEM((64, 512), BF16), f32(1, 512),
             pltpu.VMEM((1, 512), I32), pltpu.VMEM((1, 512), I32),
@@ -468,14 +514,15 @@
             f32(2, 16, 128), f32(LON - 1, 16, 128),
             f32(TILES, 9, 128), f32(TILES, 9, 128),
             f32(8, 2, 4, TX, TY), f32(8, 4, TX, TY),
-            f32(2, 4, 4, TX, TY), f32(Y - 1, 2, 4, TX, TY),
-            f32(2, 4, TX, TY), f32(4, TX, TY),
+            f32(2, 4, 4, TX, TY), f32(2 * (Y - 1), 4, TX, TY),
+            f32(4, TX, TY), f32(4, TX, TY),
             f32(2, 32, 128), f32(2, 32, 128), f32(2, 1024), f32(3, 2, 2, 1024),
             f32(LON, 1, 128), f32(ZH * LON, 1, 128), f32(8, 128),
-            f32(Y * C - 1, 8, 128), f32(8, 128), f32(LAT - 1, 8, 128),
-            sem(8), *pairs(LAT - 1), *pairs(LON - 1), *pairs(TILES - 1), *pairs(4),
-            *pairs(Y - 1), *pairs(1), *pairs(2), *pairs(3, 2), *pairs(ZH * LON - 1),
-            *pairs(Y * C - 1), *pairs(LAT - 1),
+            f32(LAT, 2, 128), f32(LAT * Y * C, 2, 128),
+            f32(4, TX, TY), f32(1, 512),
+            sem(10), *pairs(LAT - 1), *pairs(LON - 1), *pairs(TILES - 1), *pairs(4),
+            *pairs(2 * (Y - 1)), *pairs(1), *pairs(2), *pairs(3, 2), *pairs(ZH * LON - 1),
+            *pairs(LAT * Y * C - 1),
         ],
         compiler_params=pltpu.CompilerParams(
             collective_id=0, has_side_effects=True, vmem_limit_bytes=60_000_000
@@ -492,6 +539,17 @@
         control,
         perturbation,
     )
+    increment, departures = pl.pallas_call(
+        deliver,
+        out_shape=(
+            jax.ShapeDtypeStruct((4, TX, TY), F32),
+            jax.ShapeDtypeStruct((1, 512), F32),
+        ),
+        in_specs=[hbm] * 2,
+        out_specs=(hbm, hbm),
+        scratch_shapes=[f32(4, TX, TY), f32(1, 512), sem(4)],
+        name="deliver",
+    )(increment, departures)
     return increment, departures.reshape(512)
 
 

time: 58.5 us -> 56.3 us (0.962)
  local copies, waits for them, and re-layouts: 2.72 us -> 0 us
  Pallas kernels: 54.2 us -> 54.8 us
    unnamed x2 -> x0, local copies, waits for them, and re-layouts: 2.72 us -> none
    pallas_call x0 -> x1, Pallas kernels: none -> 1.51 us  [per_device(): pl.pallas_call(deliver, out_shape=(jax.ShapeDtypeStruct((4, TX, TY), F32)...]
    pallas_call x1, Pallas kernels: 54.2 us -> 53.3 us  [per_device(): pl.pallas_call(kernel, out_shape=(jax.ShapeDtypeStruct((4, TX, TY), F32),...]
where the time goes in v3:
time: 56.3 us; the launch traced here: 56.1 us
  Pallas kernels  54.8 us (97%)
  between operations  1.29 us (2%)
    pallas_call x1, Pallas kernels, per_device(): pl.pallas_call(kernel, out_shape=(jax.ShapeDtypeStruct((4, TX, TY), F32),...  53.3 us
    pallas_call x1, Pallas kernels, per_device(): pl.pallas_call(deliver, out_shape=(jax.ShapeDtypeStruct((4, TX, TY), F32)...  1.51 us

profile of v3, /device:TPU:1, one launch (start us, length us, event | category | flops | bytes accessed | tf_op | source)
XLA Modules:
  0.0 56.1 jit_solution(9692483732405478953)
XLA Ops:
  1.3 53.3 %hybrid.1 = (f32[4,32,128]{2,1,0:T(8,128)}, f32[1,512]{1,0:T(1,128)}) custom-call(f32[1,16]{1,0:T(1,128)} %bitcast.12, f32[16,64]{1,0:T(8,128)} %bitcast.8, bf16[64,512]{1,0:T(8,128)(2,1)} %bitcast.7, f32[1,512]{1,0:T(1,128)} %bitcast.9, s32[1,512]{1,0:T(1,128)} %bitcast.10, s32[1,512]{1,0:T(1,128)} %bitcast.11, s32[1]{0:T(128)S(6)} %copy.11.count, ...), custom_call_target="tpu_custom_call" | custom-call | tf_op jit(solution)/shard_map/hybrid/pallas_call | solution.py:500
  54.6 1.5 %deliver.1 = (f32[4,32,128]{2,1,0:T(8,128)}, f32[1,512]{1,0:T(1,128)}) custom-call(f32[4,32,128]{2,1,0:T(8,128)} %get-tuple-element.6.increment, f32[1,512]{1,0:T(1,128)} %get-tuple-element.7.departures), custom_call_target="tpu_custom_call" | custom-call | tf_op jit(solution)/shard_map/deliver/pallas_call | solution.py:542

commit v4 on v3

--- a/solution.py
+++ b/solution.py
@@ -46,9 +46,9 @@
     inc_hbm, dep_hbm,
     length, modes, weights, innovation, tgt, col,
     ctrl, pert, field, lat_send, lat_recv, lon_send, lon_recv, pk_send, pk_recv,
-    total, core_recv, red1, y_recv, red2, z_recv,
+    pk_all, w_all, blended, total, core_recv, red1, y_recv, red2, z_recv,
     row_send, row_recv, edge_send, edge_recv, val, val_recv, vsum, last_send, last_recv, inc_ref, dep_ref,
-    load_sem, lat_s, lat_r, lon_s, lon_r, pk_s, pk_r, core_s, core_r, y_s, y_r, z_s, z_r,
+    load_sem, lat_s, lat_r, lon_s, lon_r, pk_s, pk_r, share_s, share_r, core_s, core_r, y_s, y_r, z_s, z_r,
     row_s, row_r, edge_s, edge_r, val_s, val_r, last_s, last_r,
 ):
     mem, a, b = (lax.axis_index(n) for n in ("mem", "lat", "lon"))
@@ -120,6 +120,48 @@
         )
         copy.start()
         lat_copies.append(copy)
+
+    for load in loads[2:5]:
+        load.wait()
+    t = tgt[...]
+    rel = (((t >> 3) + (LAT - a)) & 3) * LON + (((t & 7) + (LON - b)) & 7)
+    marks = jnp.where(iota((TILES, 512), 0) == rel, 1.0, 0.0)
+    before = jnp.where(iota((512, 512), 0) < iota((512, 512), 1), 1.0, 0.0).astype(BF16)
+    rank = jnp.sum(dot(marks.astype(BF16), before) * marks, axis=0, keepdims=True).astype(I32)
+    slot = rel * 32 + rank
+    chosen = jnp.where(iota((1024, 512), 0) == slot, 1.0, 0.0).astype(BF16)
+    share = y * 8 + iota((8, 64), 0)
+    level = (share >> 2) * 8 + c * 4 + (share & 3)
+    own = jnp.where(iota((8, 64), 1) == level, 1.0, 0.0).astype(BF16)
+    picked = dot(own, weights[...])
+    place = col[...]
+    r8 = iota((8, 512), 0)
+    places = jnp.where(r8 == 0, (place >> 7).astype(F32), (place & 127).astype(F32))
+    packed = dot_nt(jnp.concatenate([picked, places], 0).astype(BF16), chosen)
+    spot = jnp.broadcast_to(packed[8:9] * 128.0 + packed[9:10], (8, 1024))
+    group = iota((8, 128), 1) >> 5
+    kept = group == (iota((8, 128), 0) & 3)
+
+    def turned(v, quarters):
+        return pltpu.roll(v, 32 * (quarters % 4), 1) if quarters % 4 else v
+
+    for k in range(TILES):
+        block, j = slice(k // 4 * 128, k // 4 * 128 + 128), k % 4
+        tile = jnp.zeros((8, 128), F32)
+        for g in range(4):
+            tile = jnp.where(kept & (group == g), turned(packed[0:8, block], g - j), tile)
+        into = pk_send if k else pk_recv
+        into[k, 0:2, :] = jnp.sum(tile.reshape(2, 4, 128), axis=1)
+        into[k, 2:3, :] = turned(spot[:, block], -j)[0:1]
+
+    pk_copies = []
+    for k in range(1, TILES):
+        copy = remote(
+            pk_send.at[k], pk_recv.at[k], pk_s.at[k - 1], pk_r.at[k - 1],
+            (mem, (a + k // LON) % LAT, (b + k % LON) % LON),
+        )
+        copy.start()
+        pk_copies.append(copy)
 
     for g in range(2):
         il = il_kx[0:1, g * 256 : (g + 1) * 256]
@@ -171,47 +213,6 @@
         copy.start()
         lon_copies.append(copy)
 
-    for load in loads[2:5]:
-        load.wait()
-    t = tgt[...]
-    rel = (((t >> 3) + (LAT - a)) & 3) * LON + (((t & 7) + (LON - b)) & 7)
-    marks = jnp.where(iota((TILES, 512), 0) == rel, 1.0, 0.0)
-    before = jnp.where(iota((512, 512), 0) < iota((512, 512), 1), 1.0, 0.0).astype(BF16)
-    rank = jnp.sum(dot(marks.astype(BF16), before) * marks, axis=0, keepdims=True).astype(I32)
-    slot = rel * 32 + rank
-    chosen = jnp.where(iota((1024, 512), 0) == slot, 1.0, 0.0).astype(BF16)
-    r32 = iota((32, 64), 0)
-    level = (r32 >> 2) * 8 + c * 4 + (r32 & 3)
-    own = jnp.where(iota((32, 64), 1) == level, 1.0, 0.0).astype(BF16)
-    picked = dot(own, weights[...])
-    place = col[...]
-    r8 = iota((8, 512), 0)
-    places = jnp.where(r8 == 0, (place >> 7).astype(F32), (place & 127).astype(F32))
-    packed = dot_nt(jnp.concatenate([picked, places], 0).astype(BF16), chosen)
-    spot = jnp.broadcast_to(packed[32:33] * 128.0 + packed[33:34], (8, 1024))
-    group = iota((8, 128), 1) >> 5
-
-    def turned(v, quarters):
-        return pltpu.roll(v, 32 * (quarters % 4), 1) if quarters % 4 else v
-
-    for k in range(TILES):
-        block, j = slice(k // 4 * 128, k // 4 * 128 + 128), k % 4
-        tile = turned(packed[0:8, block], -j)
-        for g in range(1, 4):
-            tile = jnp.where(group == g, turned(packed[8 * g : 8 * g + 8, block], g - j), tile)
-        into = pk_send if k else pk_recv
-        into[k, 0:8, :] = tile
-        into[k, 8:9, :] = turned(spot[:, block], -j)[0:1]
-
-    pk_copies = []
-    for k in range(1, TILES):
-        copy = remote(
-            pk_send.at[k], pk_recv.at[k], pk_s.at[k - 1], pk_r.at[k - 1],
-            (mem, (a + k // LON) % LAT, (b + k % LON) % LON),
-        )
-        copy.start()
-        pk_copies.append(copy)
-
     y1, y2 = iota((TY, TY), 0).astype(F32), iota((TY, TY), 1).astype(F32)
     for k in range(16):
         il = ilb[k : k + 1]
@@ -252,6 +253,17 @@
             jnp.where(row8 == 0, cl[k : k + 1], jnp.where(row8 == 1, cr[k : k + 1], 0.0))
         )
         field[k] = field[k] + (dot_tn(ch, ah) + dot_tn(co, ah) + dot_tn(ch, al))
+
+    for copy in pk_copies:
+        copy.wait_recv()
+    share_copies = []
+    for d in range(1, Y):
+        copy = remote(
+            pk_recv, pk_all.at[d - 1], share_s.at[d - 1], share_r.at[d - 1],
+            ((zh * Y + (y + d) % Y) * C + c, a, b),
+        )
+        copy.start()
+        share_copies.append(copy)
 
     loads[7].wait()
     core_copies = []
@@ -329,18 +341,10 @@
     for copy, sends, _ in halo:
         pl.when(sends)(copy.start)
 
-    w_all, p_all = [jnp.zeros((64, 128), F32)] * 4, jnp.zeros((8, 128), F32)
-    g64 = iota((64, 128), 1) >> 5
+    p_all = jnp.zeros((8, 128), F32)
     for da in range(LAT):
-        for k in range(max(1, da * LON), (da + 1) * LON):
-            pk_copies[k - 1].wait_recv()
-        got = pk_recv[da * LON : (da + 1) * LON, 0:8, :].reshape(64, 128)
-        w_all = [
-            jnp.where(g64 == da, turned(got, da - g), w) for g, w in enumerate(w_all)
-        ]
-        p_all = jnp.where(
-            group == da, turned(pk_recv[da * LON : (da + 1) * LON, 8, :], da), p_all
-        )
+        got = pk_recv[da * LON : (da + 1) * LON, 2, :]
+        p_all = jnp.where(group == da, turned(got, da), p_all)
     ys, xs = iota((TY, 128), 0), iota((TX, 128), 0)
 
     def blend(near, far, at):
@@ -358,6 +362,17 @@
         inner = jnp.sum(inner.reshape(32, TX, 128) * rows[None], axis=1)
         around = [blend(ny, fy, -1), blend(ny, fy, TY), blend(nx, fx, -1), blend(nx, fx, TX)]
         spots.append((inner, cols, rows.astype(BF16), *around))
+
+    for d in range(Y):
+        if d:
+            share_copies[d - 1].wait_recv()
+        source = pk_all.at[d - 1] if d else pk_recv
+        for r in range(8):
+            w = jnp.zeros((8, 128), F32)
+            for da in range(LAT):
+                got = source[da * LON : (da + 1) * LON, r // 4, :]
+                w = jnp.where(group == da, turned(got, da - r % 4), w)
+            w_all[d, :, r, :] = w
 
     for copy, _, gets in halo:
         pl.when(gets)(copy.wait_recv)
@@ -388,8 +403,9 @@
         down = ud[64:96] + ud[96:128] + corner[2] * west + corner[3] * east
         inner = inner + (lr[0:32] + lr[32:64]) * west + (lr[64:96] + lr[96:128]) * east
         inner = inner + up * north + down * south
-        w = jnp.concatenate([w[db * 8 : db * 8 + 8] for w in w_all], 0)
-        val[db] = jnp.sum(inner * w, axis=0, keepdims=True)
+        blended[db] = inner.reshape(Y, 8, 128)
+        parts = [w_all[d, db] * blended[db, (y + Y - d) % Y] for d in range(Y)]
+        val[db] = jnp.sum(sum(parts), axis=0, keepdims=True)
         for zo in range(ZH):
             n = zo * LON + db
             if n:
@@ -415,7 +431,6 @@
     for db in range(LON):
         vsum[db : db + 1, :] = val_recv[db] + val_recv[LON + db]
     both = vsum[...]
-    kept = group == (iota((8, 128), 0) & 3)
     for da in range(LAT):
         mine = jnp.zeros((8, 128), F32)
         for g in range(4):
@@ -468,7 +483,7 @@
 
     for copy in (*lat_copies, *lon_copies, *pk_copies, *core_copies, *y_copies, z_copy):
         copy.wait_send()
-    for copy in (*val_copies, *last_copies):
+    for copy in (*share_copies, *val_copies, *last_copies):
         copy.wait_send()
     for copy, sends, _ in halo:
         pl.when(sends)(copy.wait_send)
@@ -512,7 +527,8 @@
             f32(16, 128, TY),
             f32(2, 4, 16, TY), f32(LAT - 1, 4, 16, TY),
             f32(2, 16, 128), f32(LON - 1, 16, 128),
-            f32(TILES, 9, 128), f32(TILES, 9, 128),
+            f32(TILES, 3, 128), f32(TILES, 3, 128),
+            f32(Y - 1, TILES, 3, 128), f32(Y, LON, 8, 128), f32(LON, Y, 8, 128),
             f32(8, 2, 4, TX, TY), f32(8, 4, TX, TY),
             f32(2, 4, 4, TX, TY), f32(2 * (Y - 1), 4, TX, TY),
             f32(4, TX, TY), f32(4, TX, TY),
@@ -520,7 +536,8 @@
             f32(LON, 1, 128), f32(ZH * LON, 1, 128), f32(8, 128),
             f32(LAT, 2, 128), f32(LAT * Y * C, 2, 128),
             f32(4, TX, TY), f32(1, 512),
-            sem(10), *pairs(LAT - 1), *pairs(LON - 1), *pairs(TILES - 1), *pairs(4),
+            sem(10), *pairs(LAT - 1), *pairs(LON - 1), *pairs(TILES - 1),
+            *pairs(Y - 1), *pairs(4),
             *pairs(2 * (Y - 1)), *pairs(1), *pairs(2), *pairs(3, 2), *pairs(ZH * LON - 1),
             *pairs(LAT * Y * C - 1),
         ],

time: 56.3 us -> 53.5 us (0.950)
  Pallas kernels: 54.8 us -> 52 us
    pallas_call x1, Pallas kernels: 53.3 us -> 50.5 us  [per_device(): pl.pallas_call(kernel, out_shape=(jax.ShapeDtypeStruct((4, TX, TY), F32),...]
where the time goes in v4:
time: 53.5 us; the launch traced here: 53.3 us
  Pallas kernels  52 us (97%)
  between operations  1.29 us (2%)
    pallas_call x1, Pallas kernels, per_device(): pl.pallas_call(kernel, out_shape=(jax.ShapeDtypeStruct((4, TX, TY), F32),...  50.5 us
    pallas_call x1, Pallas kernels, per_device(): pl.pallas_call(deliver, out_shape=(jax.ShapeDtypeStruct((4, TX, TY), F32)...  1.51 us

profile of v4, /device:TPU:1, one launch (start us, length us, event | category | flops | bytes accessed | tf_op | source)
XLA Modules:
  0.0 53.3 jit_solution(15804846240414472710)
XLA Ops:
  1.3 50.5 %hybrid.1 = (f32[4,32,128]{2,1,0:T(8,128)}, f32[1,512]{1,0:T(1,128)}) custom-call(f32[1,16]{1,0:T(1,128)} %bitcast.12, f32[16,64]{1,0:T(8,128)} %bitcast.8, bf16[64,512]{1,0:T(8,128)(2,1)} %bitcast.7, f32[1,512]{1,0:T(1,128)} %bitcast.9, s32[1,512]{1,0:T(1,128)} %bitcast.10, s32[1,512]{1,0:T(1,128)} %bitcast.11, s32[1]{0:T(128)S(6)} %copy.11.count, ...), custom_call_target="tpu_custom_call" | custom-call | tf_op jit(solution)/shard_map/hybrid/pallas_call | solution.py:515
  51.8 1.5 %deliver.1 = (f32[4,32,128]{2,1,0:T(8,128)}, f32[1,512]{1,0:T(1,128)}) custom-call(f32[4,32,128]{2,1,0:T(8,128)} %get-tuple-element.6.increment, f32[1,512]{1,0:T(1,128)} %get-tuple-element.7.departures), custom_call_target="tpu_custom_call" | custom-call | tf_op jit(solution)/shard_map/deliver/pallas_call | solution.py:559

commit v5 on v4

--- a/solution.py
+++ b/solution.py
@@ -84,6 +84,9 @@
         greet((zh * Y * C + (q + d) % (Y * C), a, b))
     for d in range(LON):
         greet(((mem + Y * C) % (ZH * Y * C), a, (b + d) % LON))
+    for da in (LAT - 1, 0, 1):
+        for db in (LON - 1, 1):
+            greet((mem + 1 - 2 * c, (a + da) % LAT, (b + db) % LON))
     for da in range(1, LAT):
         for d in range(1, Y * C):
             greet((zh * Y * C + (q + d) % (Y * C), (a + da) % LAT, b))
@@ -111,7 +114,7 @@
             lat_send[0, m, g * 8 : (g + 1) * 8, :] = e[0:8]
             lat_send[1, m, g * 8 : (g + 1) * 8, :] = e[8:16]
 
-    pl.semaphore_wait(barrier, TILES - 1 + LAT * (Y * C - 1) + LON)
+    pl.semaphore_wait(barrier, TILES - 1 + LAT * (Y * C - 1) + LON + 6)
     lat_copies = []
     for d in range(1, LAT):
         copy = remote(
@@ -292,6 +295,40 @@
         copy.start()
         core_copies.append(copy)
 
+    lane = iota((8, 128), 1)
+    r8 = iota((8, 128), 0)
+    ends = jnp.where(
+        (r8 == 0) & (lane == 0) | (r8 == 1) & (lane == 127), 1.0, 0.0
+    ).astype(BF16)
+    halo = []
+    for p, (core, dev) in enumerate(((c, mem), (1 - c, mem + 1 - 2 * c))):
+        row_send[p, 0] = total[:, core, :, TX - 1, :].reshape(32, 128)
+        row_send[p, 1] = total[:, core, :, 0, :].reshape(32, 128)
+        bh, bl = halves(total[:, core].reshape(1024, 128))
+        edge_send[p] = (dot_nt(ends, bh) + dot_nt(ends, bl))[0:2]
+        for s in range(2):
+            step = 1 - 2 * s
+            copy = remote(
+                row_send.at[p, s], row_recv.at[p, s], row_s.at[p, s], row_r.at[p, s],
+                (dev, (a + step + LAT) % LAT, b),
+            )
+            there, back = a + step, a - step
+            halo.append((copy, (there >= 0) & (there < LAT), (back >= 0) & (back < LAT)))
+        for i, da in enumerate((-1, 0, 1)):
+            for j, db in enumerate((-1, 1)):
+                copy = remote(
+                    edge_send.at[p], edge_recv.at[p, i, j], edge_s.at[p, i, j],
+                    edge_r.at[p, i, j], (dev, (a - da + LAT) % LAT, (b - db + LON) % LON),
+                )
+                at, bt, af, bf = a - da, b - db, a + da, b + db
+                halo.append((
+                    copy,
+                    (at >= 0) & (at < LAT) & (bt >= 0) & (bt < LON),
+                    (af >= 0) & (af < LAT) & (bf >= 0) & (bf < LON),
+                ))
+    for copy, sends, _ in halo:
+        pl.when(sends)(copy.start)
+
     for copy in core_copies:
         copy.wait_recv()
     whole = total[:, c] + core_recv[...]
@@ -308,38 +345,7 @@
             copy.start()
             y_copies.append(copy)
 
-    lane = iota((8, 128), 1)
-    r8 = iota((8, 128), 0)
-    ends = jnp.where(
-        (r8 == 0) & (lane == 0) | (r8 == 1) & (lane == 127), 1.0, 0.0
-    ).astype(BF16)
     wh, wl = halves(whole.reshape(1024, 128))
-    row_send[0] = red1[:, :, :, TX - 1, :].reshape(32, 128)
-    row_send[1] = red1[:, :, :, 0, :].reshape(32, 128)
-    edge_send[...] = (dot_nt(ends, wh) + dot_nt(ends, wl))[0:2]
-    halo = []
-    for s in range(2):
-        step = 1 - 2 * s
-        copy = remote(
-            row_send.at[s], row_recv.at[s], row_s.at[s], row_r.at[s],
-            (mem, (a + step + LAT) % LAT, b),
-        )
-        there, back = a + step, a - step
-        halo.append((copy, (there >= 0) & (there < LAT), (back >= 0) & (back < LAT)))
-    for i, da in enumerate((-1, 0, 1)):
-        for j, db in enumerate((-1, 1)):
-            copy = remote(
-                edge_send, edge_recv.at[i, j], edge_s.at[i, j], edge_r.at[i, j],
-                (mem, (a - da + LAT) % LAT, (b - db + LON) % LON),
-            )
-            at, bt, af, bf = a - da, b - db, a + da, b + db
-            halo.append((
-                copy,
-                (at >= 0) & (at < LAT) & (bt >= 0) & (bt < LON),
-                (af >= 0) & (af < LAT) & (bf >= 0) & (bf < LON),
-            ))
-    for copy, sends, _ in halo:
-        pl.when(sends)(copy.start)
 
     p_all = jnp.zeros((8, 128), F32)
     for da in range(LAT):
@@ -376,21 +382,23 @@
 
     for copy, _, gets in halo:
         pl.when(gets)(copy.wait_recv)
-    beyond = jnp.concatenate([*halves(row_recv[0]), *halves(row_recv[1])], 0)
+    beyond = [halves(row_recv[0, n] + row_recv[1, n]) for n in range(2)]
+    beyond = jnp.concatenate([*beyond[0], *beyond[1]], 0)
+    edges = edge_recv[0] + edge_recv[1]
     z32, l32 = iota((32, 1024), 0), iota((32, 1024), 1)
     fold = jnp.where(iota((1024, TX), 0) & 31 == iota((1024, TX), 1), 1.0, 0.0).astype(BF16)
 
     def at_level(line, where):
         return jnp.where(where, line, 0.0)
 
-    left, right = edge_recv[1, 0][1:2], edge_recv[1, 1][0:1]
+    left, right = edges[1, 0][1:2], edges[1, 1][0:1]
     same = l32 >> 5 == z32
     beside = jnp.concatenate(
         [*halves(at_level(left, same)), *halves(at_level(right, same))], 0
     )
     beside = dot(beside, fold).astype(BF16)
     corner = [
-        jnp.sum(at_level(edge_recv[i, j][1 - j : 2 - j], l32 == z32 * 32 + x), 1, keepdims=True)
+        jnp.sum(at_level(edges[i, j][1 - j : 2 - j], l32 == z32 * 32 + x), 1, keepdims=True)
         for i, x in ((0, TX - 1), (2, 0))
         for j in range(2)
     ]
@@ -532,13 +540,13 @@
             f32(8, 2, 4, TX, TY), f32(8, 4, TX, TY),
             f32(2, 4, 4, TX, TY), f32(2 * (Y - 1), 4, TX, TY),
             f32(4, TX, TY), f32(4, TX, TY),
-            f32(2, 32, 128), f32(2, 32, 128), f32(2, 1024), f32(3, 2, 2, 1024),
+            f32(2, 2, 32, 128), f32(2, 2, 32, 128), f32(2, 2, 1024), f32(2, 3, 2, 2, 1024),
             f32(LON, 1, 128), f32(ZH * LON, 1, 128), f32(8, 128),
             f32(LAT, 2, 128), f32(LAT * Y * C, 2, 128),
             f32(4, TX, TY), f32(1, 512),
             sem(10), *pairs(LAT - 1), *pairs(LON - 1), *pairs(TILES - 1),
             *pairs(Y - 1), *pairs(4),
-            *pairs(2 * (Y - 1)), *pairs(1), *pairs(2), *pairs(3, 2), *pairs(ZH * LON - 1),
+            *pairs(2 * (Y - 1)), *pairs(1), *pairs(2, 2), *pairs(2, 3, 2), *pairs(ZH * LON - 1),
             *pairs(LAT * Y * C - 1),
         ],
         compiler_params=pltpu.CompilerParams(

time: 53.5 us -> 54.3 us (1.015)
  no operation moved by 1% of the time
where the time goes in v5:
time: 54.3 us; the launch traced here: 53.6 us
  Pallas kernels  52.3 us (96%)
  between operations  1.29 us (2%)
    pallas_call x1, Pallas kernels, per_device(): pl.pallas_call(kernel, out_shape=(jax.ShapeDtypeStruct((4, TX, TY), F32),...  50.8 us
    pallas_call x1, Pallas kernels, per_device(): pl.pallas_call(deliver, out_shape=(jax.ShapeDtypeStruct((4, TX, TY), F32)...  1.51 us

profile of v5, /device:TPU:1, one launch (start us, length us, event | category | flops | bytes accessed | tf_op | source)
XLA Modules:
  0.0 53.6 jit_solution(6308886632624548992)
XLA Ops:
  1.3 50.8 %hybrid.1 = (f32[4,32,128]{2,1,0:T(8,128)}, f32[1,512]{1,0:T(1,128)}) custom-call(f32[1,16]{1,0:T(1,128)} %bitcast.12, f32[16,64]{1,0:T(8,128)} %bitcast.8, bf16[64,512]{1,0:T(8,128)(2,1)} %bitcast.7, f32[1,512]{1,0:T(1,128)} %bitcast.9, s32[1,512]{1,0:T(1,128)} %bitcast.10, s32[1,512]{1,0:T(1,128)} %bitcast.11, s32[1]{0:T(128)S(6)} %copy.11.count, ...), custom_call_target="tpu_custom_call" | custom-call | tf_op jit(solution)/shard_map/hybrid/pallas_call | solution.py:523
  52.1 1.5 %deliver.1 = (f32[4,32,128]{2,1,0:T(8,128)}, f32[1,512]{1,0:T(1,128)}) custom-call(f32[4,32,128]{2,1,0:T(8,128)} %get-tuple-element.6.increment, f32[1,512]{1,0:T(1,128)} %get-tuple-element.7.departures), custom_call_target="tpu_custom_call" | custom-call | tf_op jit(solution)/shard_map/deliver/pallas_call | solution.py:567
